TPU v7x, 128 devices: a 2x2x16 block of a 8x8x16 slice. The times are simulated.
128 devices in a mesh: groups: 4 (over x, y), seq: 16 (over z), tensor: 2 (over core).
Axes of the slice: x: 2, y: 2, z: 16, core: 2. Of those that a mesh axis runs over, the one named last changes fastest.
The devices are a block of a 8x8x16 slice.
Arguments:
- patches: bfloat16 [24576, 1152], P(('groups', 'seq')), parts along dimension 0, may hold values from -6 to 6
- vis_up: bfloat16 [1152, 4304], P(None, 'tensor'), may hold values from -0.1875 to 0.1875
- vis_down: bfloat16 [4304, 1152], P('tensor'), may hold values from -0.09375 to 0.09375
- merge_weight: bfloat16 [4608, 5120], P('seq', 'tensor'), may hold values from -0.09375 to 0.09375
- text_states: bfloat16 [12288, 5120], P(('groups', 'seq'), 'tensor'), parts along dimension 0, may hold values from -6 to 6
- w_query: bfloat16 [5120, 4096], P('seq', 'tensor'), may hold values from -2.5 to 2.5, as said below
- w_key: bfloat16 [5120, 512], P('seq', 'tensor'), may hold values from -2.5 to 2.5, as said below
- w_value: bfloat16 [5120, 512], P('seq', 'tensor'), may hold values from -0.078125 to 0.078125
- dest_rows: int32 [6144], P(('groups', 'seq')), parts along dimension 0, may hold values from 0 to 3071, as said below
- doc_ids: int32 [12288], P(('groups', 'seq')), parts along dimension 0, may hold values from 0 to 3, never falling along the last dimension, each value on 1 to 1536 neighbouring positions
Outputs:
- attended: bfloat16 [12288, 4096], P(('groups', 'seq'), 'tensor'), parts along dimension 0
There are 4 independent parts, one for each index of `groups`. A program takes and returns all parts, laid end to end along the dimension named above; an argument that names none is the same for every part. Nothing has to cross between parts.
Inputs may be any that keep to these rules, and one draw needn't show every extreme that they name: `dest_rows`: all entries are distinct; each text shard of 192 positions receives exactly 96 of them; at most 12 of the rows of one seq shard go to one text shard, and some pair reaches 12 in every draw. `w_query`: A query projection of order 5120 ** -0.5 per entry. `w_key`: A key projection of order 5120 ** -0.5 per entry.
All inputs are finite; a program needn't handle non-finite values.
Results may differ from a plain program's by a relative error of at most 0.03.
Values may be sent and summed in bfloat16 or wider, within the bound.
A program may use at most 128 MiB of HBM per device.

v0:
```python
import jax
import jax.numpy as jnp
from jax import lax
from jax.sharding import PartitionSpec as P

HD = 128


epsilon = 1e-06


def copy_for_each(shard, axis):
    count = lax.axis_size(axis)
    return lax.all_to_all(
        jnp.broadcast_to(shard[None], (count, *shard.shape)), axis, 0, 0, tiled=True
    )


def of_everyone(shard, axis):
    everything = copy_for_each(shard, axis)
    return jnp.sum(everything.astype(jnp.float32), axis=0)


def laid_out(tiles, dim):
    lengths = list(tiles.shape[1:])
    lengths[dim] *= tiles.shape[0]
    return jnp.moveaxis(tiles, 0, dim).reshape(lengths)


def gather_directly(shard, axis, dim):
    tiles = copy_for_each(shard, axis)
    return laid_out(tiles, dim)


def gathered_total(shard, axis):
    tiles = lax.all_gather(shard, axis)
    return tiles.sum(axis=0)


def side_by_side(arrays, axis, dim, along):
    both = jnp.concatenate(arrays, axis=along)
    out, at, outs = (lax.all_gather(both, axis, axis=dim, tiled=True), 0, [])
    for a in arrays:
        outs.append(lax.slice_in_dim(out, at, at + a.shape[along], axis=along))
        at += a.shape[along]
    return tuple(outs)


def layer_norm(values):
    center = jnp.mean(values, axis=-1, keepdims=True)
    spread = jnp.mean((values - center) ** 2, axis=-1, keepdims=True)
    return (values - center) * lax.rsqrt(spread + epsilon)


def body(
    patches,
    vis_up,
    vis_down,
    merge_weight,
    text_states,
    w_query,
    w_key,
    w_value,
    dest_rows,
    doc_ids,
):
    patch_rows = patches.shape[0]
    values = patches.astype(jnp.float32)
    normed = layer_norm(values).astype(jnp.bfloat16)
    activated = jax.nn.gelu(
        jnp.dot(normed, vis_up, preferred_element_type=jnp.float32), approximate=True
    ).astype(jnp.bfloat16)
    vision_out = values + of_everyone(
        jnp.dot(activated, vis_down, preferred_element_type=jnp.float32).astype(jnp.bfloat16),
        "tensor",
    ).astype(jnp.float32)
    merged_rows = patch_rows // 4
    grouped = layer_norm(vision_out.reshape(merged_rows, 4 * vision_out.shape[1])).astype(
        jnp.bfloat16
    )
    columns = lax.all_to_all(grouped, "seq", split_axis=1, concat_axis=0, tiled=True)
    seq_index = lax.axis_index("seq")
    text_rows = text_states.shape[0]
    half_width = text_states.shape[1]
    destinations = gather_directly(dest_rows, "seq", 0)
    ordering = jnp.argsort(destinations, stable=True)
    in_order = jnp.take(columns, ordering, axis=0)
    sorted_dest = jnp.take(destinations, ordering, axis=0)
    piece = in_order
    owned_rows = lax.psum_scatter(
        jnp.dot(piece, merge_weight, preferred_element_type=jnp.float32).astype(jnp.bfloat16),
        "seq",
        scatter_dimension=0,
        tiled=True,
    )
    landing = (
        lax.dynamic_slice_in_dim(sorted_dest, seq_index * merged_rows, merged_rows, 0)
        - seq_index * text_rows
    )
    placer = (jnp.arange(text_rows, dtype=jnp.int32)[:, None] == landing[None, :]).astype(
        jnp.bfloat16
    )
    routed = jnp.dot(placer, owned_rows, preferred_element_type=jnp.float32)
    mixed_text = text_states.astype(jnp.float32) + routed
    squares = gathered_total(jnp.sum(mixed_text * mixed_text, axis=1), "tensor")
    full_width = lax.axis_size("tensor") * half_width
    normed_text = (mixed_text * lax.rsqrt(squares / full_width + epsilon)[:, None]).astype(
        jnp.bfloat16
    )
    features = gather_directly(normed_text, "tensor", 1)
    query_cols = w_query.shape[1]
    kv_cols = w_key.shape[1]
    initial = (
        jnp.zeros((text_rows, query_cols), jnp.float32),
        jnp.zeros((text_rows, kv_cols), jnp.float32),
        jnp.zeros((text_rows, kv_cols), jnp.float32),
    )
    pieces = side_by_side((w_query, w_key, w_value), "seq", 0, 1)
    query_sum, key_sum, value_sum = tuple(
        (jnp.dot(features, piece, preferred_element_type=jnp.float32) for piece in pieces)
    )
    queries = query_sum.astype(jnp.bfloat16)
    key_proj = key_sum.astype(jnp.bfloat16)
    value_proj = value_sum.astype(jnp.bfloat16)
    heads_local = query_cols // HD
    kv_local = kv_cols // HD
    group_size = heads_local // kv_local
    score_scale = HD ** (-0.5)
    query_blocks = queries.reshape(text_rows, kv_local, group_size, HD)
    first_row = seq_index * text_rows
    query_positions = first_row + jnp.arange(text_rows, dtype=jnp.int32)

    def update(previous, key_piece, value_piece, doc_piece, start):
        previous_top, weight_sum, accumulated = previous
        piece_rows = key_piece.shape[0]
        key_positions = start + jnp.arange(piece_rows, dtype=jnp.int32)
        visible = (key_positions[None, :] <= query_positions[:, None]) & (
            doc_piece[None, :] == doc_ids[:, None]
        )
        visible = visible[:, None, None, :]
        scores = (
            jnp.einsum(
                "tkgd,skd->tkgs",
                query_blocks,
                key_piece.reshape(piece_rows, kv_local, HD),
                preferred_element_type=jnp.float32,
            )
            * score_scale
        )
        highest = jnp.maximum(previous_top, jnp.max(jnp.where(visible, scores, -1e30), axis=-1))
        raw = jnp.where(visible, jnp.exp(scores - highest[..., None]), 0.0)
        factor = jnp.exp(previous_top - highest)
        new_sum = weight_sum * factor + jnp.sum(raw, axis=-1)
        added = jnp.einsum(
            "tkgs,skd->tkgd",
            raw.astype(jnp.bfloat16),
            value_piece.reshape(piece_rows, kv_local, HD),
            preferred_element_type=jnp.float32,
        )
        return (highest, new_sum, accumulated * factor[..., None] + added)

    initial = (
        jnp.full((text_rows, kv_local, group_size), -1e30, jnp.float32),
        jnp.zeros((text_rows, kv_local, group_size), jnp.float32),
        jnp.zeros((text_rows, kv_local, group_size, HD), jnp.float32),
    )
    key_piece, value_piece, doc_piece = (
        *side_by_side((key_proj, value_proj), "seq", 0, 1),
        lax.all_gather(doc_ids, "seq", axis=0, tiled=True),
    )
    piece_rows = key_piece.shape[0]
    key_block = 512
    block_count = piece_rows // key_block

    def visit(previous):
        keys_split = key_piece.reshape(block_count, key_block, key_piece.shape[1])
        values_split = value_piece.reshape(block_count, key_block, value_piece.shape[1])
        docs_split = doc_piece.reshape(block_count, key_block)
        starts = key_block * jnp.arange(block_count, dtype=jnp.int32)

        def step_keys(carried, items):
            return (update(carried, items[0], items[1], items[2], items[3]), None)

        finished, _ = lax.scan(step_keys, previous, (keys_split, values_split, docs_split, starts))
        return finished

    def skipped(previous):
        return previous

    final_top, weight_sum, accumulated = lax.cond(
        jnp.int32(0) <= first_row + text_rows - 1, visit, skipped, initial
    )
    return (accumulated / weight_sum[..., None]).reshape(text_rows, query_cols).astype(jnp.bfloat16)


def solution(mesh):
    in_specs = (
        P(("groups", "seq"), None),
        P(None, "tensor"),
        P("tensor", None),
        P("seq", "tensor"),
        P(("groups", "seq"), "tensor"),
        P("seq", "tensor"),
        P("seq", "tensor"),
        P("seq", "tensor"),
        P(("groups", "seq")),
        P(("groups", "seq")),
    )
    out_specs = P(("groups", "seq"), "tensor")
    return jax.shard_map(body, mesh=mesh, in_specs=in_specs, out_specs=out_specs, check_vma=False)
```

profile of v0, /device:TPU:1604, one launch (start us, length us, event | category | flops | bytes accessed | tf_op | source)
XLA Modules:
  0.0 689.2 jit_solution(16462914497833231736)
XLA Ops:
  6.6 1.5 convert_reduce_fusion.1
  8.0 1.5 fusion.37
  9.6 10.4 %convolution_convert_fusion.1 = bf16[384,1152]{1,0:T(8,128)(2,1)S(1)} fusion(bf16[2152,1152]{1,0:T(8,128)(2,1)} %param.16, bf16[1152,2152]{0,1:T(8,128)(2,1)} %param.15, bf16[384,1152]{1,0:T(8,128)(2,1)} %param.14, f32[384]{0:T(512)S(1)} %add_rsqrt_fusion, f32[384]{0:T(512)S(1)} %broadcast_multiply_fusion), kind=kOutput, calls=%fused_computation.43 | convolution fusion | flops 3817552896 | bytes 11688960 | tf_op jit(solution)/shard_map/dot_general | solution.py:74
  20.2 5.2 all_to_all.32
  25.9 9.4 %all-to-all-start = ((s32[16,1,96]{2,1,0:T(1,128)}), s32[16,1,96]{2,1,0:T(1,128)S(1)}, u32[]{:S(2)}, u32[]{:S(2)}) async-start(s32[16,1,96]{2,1,0:T(1,128)} %broadcast_in_dim.84), calls=%async_computation | async-start | bytes 16384 | tf_op jit(solution)/shard_map/all_to_all | solution.py:14
  35.7 1.5 fusion.70
  37.6 2.6 reshape.149
  40.7 3.5 fusion.34
  44.2 12.0 %all-to-all-start.2 = ((bf16[96,16,288]{2,0,1:T(8,128)(2,1)}), bf16[96,16,288]{2,0,1:T(8,128)(2,1)S(1)}, u32[]{:S(2)}, u32[]{:S(2)}) async-start(bf16[96,16,288]{2,0,1:T(8,128)(2,1)} %fusion.34), calls=%async_computation.2 | async-start | bytes 2359296 | tf_op jit(solution)/shard_map/all_to_all | solution.py:81
  57.7 5.0 sort.17
  62.8 46.7 %all-to-all-done.2 = bf16[96,16,288]{2,0,1:T(8,128)(2,1)S(1)} async-done(((bf16[96,16,288]{2,0,1:T(8,128)(2,1)}), bf16[96,16,288]{2,0,1:T(8,128)(2,1)S(1)}, u32[]{:S(2)}, u32[]{:S(2)}) %all-to-all-start.2) | async-done | bytes 884768 | tf_op jit(solution)/shard_map/all_to_all | solution.py:81
  109.5 5.3 gather_fusion.1
  114.8 7.7 %convolution_convert_fusion = bf16[1536,2560]{1,0:T(8,128)(2,1)} fusion(bf16[288,2560]{1,0:T(8,128)(2,1)S(1)} %copy-done, bf16[1536,288]{1,0:T(8,128)(2,1)} %gather_fusion.1, pred[1536]{0:T(1024)(128)(4,1)S(1)} %compare_and_fusion.1), kind=kOutput, calls=%fused_computation.31 | convolution fusion | flops 2269298688 | bytes 10225152 | tf_op jit(solution)/shard_map/dot_general | solution.py:91
  126.6 8.4 %gather_fusion = s32[1536]{0:T(1024)S(1)} fusion(s32[1536]{0:T(1024)S(1)} %reshape.148, s32[2048]{0:T(1024)S(1)} %pad_clamp_fusion), kind=kCustom, calls=%fused_computation | custom fusion | bytes 18432 | tf_op jit(solution)/shard_map/jit(_take)/gather | solution.py:88
  135.1 83.5 %reduce-scatter.2.cloned.1.call-done = bf16[96,2560]{1,0:T(8,128)(2,1)} async-done(((bf16[1536,2560]{1,0:T(8,128)(2,1)}), bf16[96,2560]{1,0:T(8,128)(2,1)}) %reduce-scatter.2.cloned.1.call-update) | async-done | bytes 491536 | tf_op jit(solution)/shard_map/reduce_scatter | solution.py:90
  218.6 1.5 multiply_reduce_fusion
  220.4 2.5 all-reduce
  223.3 5.3 all_to_all.33
  228.8 271.1 %all-gather.4.cloned.1.call-done = bf16[5120,2560]{1,0:T(8,128)(2,1)} async-done(((bf16[320,2560]{1,0:T(8,128)(2,1)}), bf16[5120,2560]{1,0:T(8,128)(2,1)}) %all-gather.4.cloned.1.call-update) | async-done | bytes 26214416 | tf_op jit(solution)/shard_map/all_gather | solution.py:42
  499.9 2.4 fusion.46
  502.3 2.4 fusion.49
  507.0 54.1 %all-reduce.1 = s32[3072]{0:T(1024)S(1)} all-reduce(s32[3072]{0:T(1024)S(1)} %dynamic-update-slice.1), channel_id=1, replica_groups=mesh['groups'=4,'seq'=16,'tensor'=2] {'seq'}, use_global_device_ids=true, to_apply=%add.1 | all-reduce | flops 3072 | bytes 24576
  561.2 11.3 %fusion.30 = bf16[192,2048]{1,0:T(8,128)(2,1)S(1)} fusion(bf16[192,5120]{1,0:T(8,128)(2,1)S(1)} %bitcast.90, bf16[5120,2560]{1,0:T(8,128)(2,1)} %all-gather.4.cloned.1.call-done), kind=kOutput, calls=%fused_computation.51 | convolution fusion | flops 4026925056 | bytes 23724032 | tf_op jit(solution)/shard_map/dot_general | solution.py:120
  572.5 1.8 all-gather.6.cloned.1.call-done
  574.3 104.7 %conditional.1 = (f32[192,2,8]{0,2,1:T(8,128)}, f32[192,2,8,128]{3,0,2,1:T(8,128)}) conditional(s32[]{:T(128)} %convert_element_type.50, () %tuple.17, (bf16[3072,512]{1,0:T(8,128)(2,1)}, s32[3072]{0:T(1024)S(1)}, s32[]{:T(128)}, s32[192]{0:T(256)S(1)}, bf16[192,2048]{1,0:T(8,128)(2,1)S(1)}, /*index=5*/s32[192]{0:T(256)S(1)}) %tuple.60), branch_computations={%region_11.12_spmd, %region_12.17_spmd} | conditional | flops 824098496 | bytes 35493180 | solution.py:190
  574.3 3.2 fusion.71
  577.9 101.1 %while.14 = (s32[]{:T(128)}, f32[192,2,8]{0,2,1:T(8,128)S(1)}, f32[192,2,8]{0,2,1:T(8,128)}, f32[192,2,8,128]{3,0,2,1:T(8,128)}, s32[6]{0:T(128)S(1)}, /*index=5...) while((s32[]{:T(128)}, f32[192,2,8]{0,2,1:T(8,128)S(1)}, ...), condition=%wide.region_16.16_spmd.clone, body=%wide.region_13.15_spmd.clone.sunk | while | flops 824098304 | bytes 26029728 | solution.py:184
  580.6 3.8 fusion.93
  584.4 3.8 fusion.94
  589.1 4.9 bitcast_add_fusion.2
  596.6 3.8 fusion.93
  600.5 3.8 fusion.94
  604.3 1.3 fusion.95
  605.8 5.2 bitcast_add_fusion.2
  613.6 3.8 fusion.93
  617.5 3.8 fusion.94
  621.3 1.3 fusion.95
  622.8 5.2 bitcast_add_fusion.2
  630.7 3.8 fusion.93
  634.5 3.8 fusion.94
  639.8 5.2 bitcast_add_fusion.2
  647.7 3.8 fusion.93
  651.5 3.8 fusion.94
  656.8 5.2 bitcast_add_fusion.2
  664.7 3.8 fusion.93
  668.5 3.8 fusion.94
  673.8 5.2 bitcast_add_fusion.2
  679.0 2.0 divide_convert_fusion
  (132 shorter events, 32.9 us)
Async XLA Ops:
  6.5 108.2 %copy-start = (bf16[288,2560]{1,0:T(8,128)(2,1)S(1)}, bf16[288,2560]{1,0:T(8,128)(2,1)}, u32[]{:S(2)}) copy-start(bf16[288,2560]{1,0:T(8,128)(2,1)} %param.17) | copy-start | bytes 4423684
  20.2 5.2 copy-start.7
  25.9 18.2 %all-to-all-start = ((s32[16,1,96]{2,1,0:T(1,128)}), s32[16,1,96]{2,1,0:T(1,128)S(1)}, u32[]{:S(2)}, u32[]{:S(2)}) async-start(s32[16,1,96]{2,1,0:T(1,128)} %broadcast_in_dim.84), calls=%async_computation | async-start | bytes 16384 | tf_op jit(solution)/shard_map/all_to_all | solution.py:14
  44.2 65.3 %all-to-all-start.2 = ((bf16[96,16,288]{2,0,1:T(8,128)(2,1)}), bf16[96,16,288]{2,0,1:T(8,128)(2,1)S(1)}, u32[]{:S(2)}, u32[]{:S(2)}) async-start(bf16[96,16,288]{2,0,1:T(8,128)(2,1)} %fusion.34), calls=%async_computation.2 | async-start | bytes 2359296 | tf_op jit(solution)/shard_map/all_to_all | solution.py:81
  56.2 162.4 %reduce-scatter.2.cloned.1.call-start = ((), (), s32[]{:S(2)}) async-start(), calls=%async_computation.5 | async-start | bytes 8355840 | tf_op jit(solution)/shard_map/reduce_scatter | solution.py:90
  122.5 1.3 copy-start.2
  122.5 1.3 copy-start.4
  122.5 1.4 copy-start.5
  122.6 2.7 copy-start.9
  122.6 377.3 %all-gather.4.cloned.1.call-start = ((), (), s32[]{:S(2)}) async-start(), calls=%async_computation.6 | async-start | bytes 27852800 | tf_op jit(solution)/shard_map/all_gather | solution.py:42
  125.2 449.0 %all-gather.6.cloned.1.call-start = ((), (), s32[]{:S(2)}) async-start(), calls=%async_computation.7 | async-start | bytes 3342336 | tf_op jit(solution)/shard_map/all_gather | solution.py:42
  126.6 92.0 %copy-start.3 = (bf16[192,2560]{1,0:T(8,128)(2,1)S(1)}, bf16[192,2560]{1,0:T(8,128)(2,1)}, u32[]{:S(2)}) copy-start(bf16[192,2560]{1,0:T(8,128)(2,1)} %param.18) | copy-start | bytes 2949124
  502.3 3.2 copy-start.8
  502.3 4.5 copy-start.6
  679.0 3.6 copy-start.1
Sparse Core Ops, SparseCore 0:
  122.7 95.8 reduce-scatter.1
  220.2 279.6 all-gather.3
  505.6 68.5 all-gather.5
where the time goes:
time: 700 us; the launch traced here: 689 us
  waiting for transfers between devices  403 us (58%)
  matrix products  89.5 us (13%)
  blocking collectives  67.1 us (10%)
  other arithmetic  54.3 us (8%)
  local copies, waits for them, and re-layouts  38.2 us (5%)
  starting transfers between devices  21.8 us (3%)
  between operations  14.7 us (2%)
    all_gather x2, waiting for transfers between devices, side_by_side(): out, at, outs = (lax.all_gather(both, axis, axis=dim, tiled=True), 0, [])  273 us
    reduce_scatter x1, waiting for transfers between devices, body(): lax.psum_scatter(jnp.dot(piece, merge_weight, preferred_element_type=jnp....  83.5 us
    unnamed x2, blocking collectives  56.6 us
    all_to_all x1, waiting for transfers between devices, body(): lax.all_to_all(grouped, 'seq', split_axis=1, concat_axis=0, tiled=True)  46.7 us
    dot_general x6, matrix products, update(): jnp.einsum('tkgs,skd->tkgd', raw.astype(jnp.bfloat16), value_piece.reshap...  30.8 us
    reduce_sum x6, other arithmetic, update(): new_sum = weight_sum * factor + jnp.sum(raw, axis=-1)  23 us
    dot_general x6, matrix products, update(): jnp.einsum('tkgd,skd->tkgs', query_blocks, key_piece.reshape(piece_rows,...  22.8 us
    dot_general x3, matrix products, body(): jnp.dot(features, piece, preferred_element_type=jnp.float32)  16.2 us
  transfers between devices with their start and end apart: 5, of which 4 were waited for; matrix products, arithmetic and copies ran while one was open for 6% of the time, Pallas kernels for 0%

commit v1 on v0

v1 whole, which is shorter than its diff:
```python
import functools
import math

import jax
import jax.numpy as jnp
from jax import lax
from jax.experimental import pallas as pl
from jax.experimental.pallas import tpu as pltpu
from jax.sharding import PartitionSpec as P

HD = 128
BLOCK = 4
REACH = 1536
CLIPS = 4
FAR = -(2.0**100)
LOG2E = 1.4426950408889634

epsilon = 1e-06


def layer_norm(values):
    center = jnp.mean(values, axis=-1, keepdims=True)
    spread = jnp.mean((values - center) ** 2, axis=-1, keepdims=True)
    return (values - center) * lax.rsqrt(spread + epsilon)


def everyones(shard, axis):
    count = lax.axis_size(axis)
    return lax.all_to_all(
        jnp.broadcast_to(shard[None], (count, *shard.shape)), axis, 0, 0, tiled=True
    )


def swap_core(x):
    return lax.ppermute(x, "tensor", [(0, 1), (1, 0)])


def block_swaps():
    groups = lax.axis_size("groups")
    wide = math.isqrt(groups)

    def partner(i, j):
        row, col = divmod(i, wide)
        return (row ^ (j >> 1)) * wide + (col ^ (j & 1))

    swaps = [[(i, partner(i, j)) for i in range(groups)] for j in range(BLOCK)]
    index = lax.axis_index("groups")
    quarter = 2 * ((index // wide) % 2) + index % 2
    return swaps, quarter


def attention_kernel(
    reach, kv_local, group, qkv_ref, doc_q_ref, doc_k_ref, out_ref,
    kv_buf, q_buf, top, total, send_sem, recv_sem,
):
    me = lax.axis_index("seq")
    count = lax.axis_size("seq")
    rows = qkv_ref.shape[1]
    MESH = pl.DeviceIdType.MESH

    barrier = pltpu.get_barrier_semaphore()

    @pl.when(me > 0)
    def _():
        pl.semaphore_signal(barrier, inc=1, device_id={"seq": me - 1}, device_id_type=MESH)

    @pl.when(me < count - 1)
    def _():
        pl.semaphore_signal(barrier, inc=1, device_id={"seq": me + 1}, device_id_type=MESH)

    for i in range(2 * kv_local):
        kv_buf[0, :, i * HD : (i + 1) * HD] = qkv_ref[i, :, :HD]

    pl.semaphore_wait(barrier, jnp.minimum(me, 1) + jnp.minimum(count - 1 - me, 1))

    half = kv_local * HD

    def pass_on(slot, part):
        cols = pl.ds(part * half, half)
        return pltpu.make_async_remote_copy(
            src_ref=kv_buf.at[slot, :, cols],
            dst_ref=kv_buf.at[slot + 1, :, cols],
            send_sem=send_sem.at[slot, part],
            recv_sem=recv_sem.at[slot, part],
            device_id={"seq": me + 1},
            device_id_type=MESH,
        )

    @pl.when(me < count - 1)
    def _():
        pass_on(0, 0).start()
        pass_on(0, 1).start()

    doc_q = doc_q_ref[...]
    per = BLOCK
    for h in range(kv_local * group):
        g, i = divmod(h, group)
        spot = pl.ds(i * rows, rows)
        k, j = divmod(h, per)
        q_buf[g, spot, :HD] = qkv_ref[k, :, (1 + j) * HD : (2 + j) * HD]
        q_buf[g, spot, HD:] = doc_q
    chunk = 2 * rows

    def visit(slot, start):
        doc_k = doc_k_ref[pl.ds(pl.multiple_of(start, rows), rows), :]
        ones = jnp.ones((rows, HD), jnp.bfloat16)

        @pl.loop(0, kv_local)
        def _(g):
            at = pl.multiple_of(g * HD, HD)
            keys = jnp.concatenate([kv_buf[slot, :, pl.ds(at, HD)], doc_k], axis=1)
            vals = jnp.concatenate([kv_buf[slot, :, pl.ds(half + at, HD)], ones], axis=1)
            for b in range(group * rows // chunk):
                spot = pl.ds(b * chunk, chunk)
                s = lax.dot_general(
                    q_buf[g, spot, :], keys, (((1,), (1,)), ((), ())),
                    preferred_element_type=jnp.float32,
                )
                first = isinstance(slot, int)
                if first:
                    token = lax.rem(
                        lax.broadcasted_iota(jnp.int32, s.shape, 0), jnp.int32(rows)
                    )
                    other = lax.broadcasted_iota(jnp.int32, s.shape, 1)
                    s = jnp.where(other <= token, s, FAR)
                    high = jnp.max(s, axis=1, keepdims=True)
                    raw = jnp.exp2(s - high).astype(jnp.bfloat16)
                    total[g, spot, :] = jnp.dot(raw, vals, preferred_element_type=jnp.float32)
                    top[g, spot, :] = high
                else:
                    before = top[g, spot, :]
                    high = jnp.maximum(before, jnp.max(s, axis=1, keepdims=True))
                    raw = jnp.exp2(s - high).astype(jnp.bfloat16)
                    total[g, spot, :] = total[g, spot, :] * jnp.exp2(before - high) + jnp.dot(
                        raw, vals, preferred_element_type=jnp.float32
                    )
                    top[g, spot, :] = high

    visit(0, me * rows)

    @pl.loop(1, reach + 1)
    def _(slot):
        @pl.when(slot <= me)
        def _():
            for part in range(2):
                pass_on(slot - 1, part).wait_recv()

                @pl.when((slot < reach) & (me < count - 1))
                def _():
                    pass_on(slot, part).start()

            visit(slot, (me - slot) * rows)

    for h in range(kv_local * group):
        g, i = divmod(h, group)
        spot = pl.ds(i * rows, rows)
        out_ref[:, h * HD : (h + 1) * HD] = (
            total[g, spot, :HD] / total[g, spot, HD:]
        ).astype(out_ref.dtype)

    @pl.loop(0, reach)
    def _(slot):
        @pl.when((slot <= me) & (me < count - 1))
        def _():
            for part in range(2):
                pass_on(slot, part).wait_send()


def attention(qkv, doc_q, doc_k, kv_local, group):
    rows = qkv.shape[1]
    reach = -(-(REACH - 1) // rows)
    vmem = pl.BlockSpec(memory_space=pltpu.VMEM)
    heads = kv_local * group
    keys = (reach + 1) * rows
    return pl.pallas_call(
        functools.partial(attention_kernel, reach, kv_local, group),
        out_shape=jax.ShapeDtypeStruct((rows, heads * HD), jnp.bfloat16),
        in_specs=[vmem] * 3,
        out_specs=vmem,
        scratch_shapes=[
            pltpu.VMEM((reach + 1, rows, 2 * kv_local * HD), jnp.bfloat16),
            pltpu.VMEM((kv_local, group * rows, 2 * HD), jnp.bfloat16),
            pltpu.VMEM((kv_local, group * rows, 1), jnp.float32),
            pltpu.VMEM((kv_local, group * rows, 2 * HD), jnp.float32),
            pltpu.SemaphoreType.DMA((reach, 2)),
            pltpu.SemaphoreType.DMA((reach, 2)),
        ],
        compiler_params=pltpu.CompilerParams(
            collective_id=0, has_side_effects=True, vmem_limit_bytes=48 << 20
        ),
        cost_estimate=pl.CostEstimate(
            flops=4 * rows * keys * heads * HD,
            bytes_accessed=8 * qkv.size,
            transcendentals=rows * keys * heads,
        ),
        name="attend",
    )(qkv, doc_q, doc_k)


def body(
    patches,
    vis_up,
    vis_down,
    merge_weight,
    text_states,
    w_query,
    w_key,
    w_value,
    dest_rows,
    doc_ids,
):
    f32, bf16 = jnp.float32, jnp.bfloat16
    swaps, quarter = block_swaps()
    core = lax.axis_index("tensor")
    seq_index = lax.axis_index("seq")
    seq_size = lax.axis_size("seq")
    text_rows, half_width = text_states.shape
    query_cols, kv_cols = w_query.shape[1], w_key.shape[1]
    kv_local = kv_cols // HD
    group = query_cols // kv_cols

    def in_block(pieces):
        return [pieces[0]] + [lax.ppermute(pieces[j], "groups", swaps[j]) for j in (1, 2, 3)]

    kv_part, q_part = 2 * kv_cols // BLOCK, query_cols // BLOCK
    w_kv = jnp.concatenate([w_key, w_value], axis=1)
    w_mine = jnp.concatenate(
        [
            lax.dynamic_slice_in_dim(w_kv, quarter * kv_part, kv_part, 1),
            lax.dynamic_slice_in_dim(w_query, quarter * q_part, q_part, 1),
        ],
        axis=1,
    )
    weights = lax.all_gather(w_mine, "seq", axis=0, tiled=True)

    ints = everyones(jnp.concatenate([dest_rows, doc_ids]), "seq")
    merged_rows = dest_rows.shape[0]
    dests, docs = ints[:, :merged_rows], ints[:, merged_rows:].reshape(-1)

    values = patches.astype(f32)
    normed = layer_norm(values).astype(bf16)
    activated = jax.nn.gelu(
        jnp.dot(normed, vis_up, preferred_element_type=f32), approximate=True
    ).astype(bf16)
    partial = jnp.dot(activated, vis_down, preferred_element_type=f32).astype(bf16)
    half_rows = patches.shape[0] // 2
    away = swap_core(lax.dynamic_slice_in_dim(partial, (1 - core) * half_rows, half_rows, 0))
    kept = lax.dynamic_slice_in_dim(partial, core * half_rows, half_rows, 0)
    vision_out = (
        lax.dynamic_slice_in_dim(patches, core * half_rows, half_rows, 0).astype(f32)
        + kept.astype(f32)
        + away.astype(f32)
    )
    grouped = layer_norm(vision_out.reshape(half_rows // 4, 4 * vision_out.shape[1])).astype(bf16)
    mine = lax.all_to_all(grouped, "seq", split_axis=1, concat_axis=0, tiled=True)
    other = swap_core(mine)
    columns = jnp.concatenate([mine, other], axis=0)
    half_merged = merged_rows // 2
    first = lax.dynamic_slice_in_dim(dests, core * half_merged, half_merged, 1).reshape(-1)
    second = lax.dynamic_slice_in_dim(dests, (1 - core) * half_merged, half_merged, 1).reshape(-1)
    dest = jnp.concatenate([first, second])
    rank = jnp.sum((dest[None, :] < dest[:, None]).astype(jnp.int32), axis=1)
    total_rows = rank.shape[0]
    order = jnp.arange(total_rows, dtype=jnp.int32)[:, None] == rank[None, :]
    in_order = jnp.dot(order.astype(bf16), columns, preferred_element_type=f32).astype(bf16)
    products = jnp.dot(in_order, merge_weight, preferred_element_type=f32).astype(bf16)
    products, weights = lax.optimization_barrier((products, weights))
    owned = lax.psum_scatter(products, "seq", scatter_dimension=0, tiled=True)

    ranks_here = seq_index * merged_rows + jnp.arange(merged_rows, dtype=jnp.int32)
    landing = (
        jnp.sum(jnp.where(ranks_here[:, None] == rank[None, :], dest[None, :], 0), axis=1)
        - seq_index * text_rows
    )
    placer = (
        jnp.arange(text_rows, dtype=jnp.int32)[:, None] == landing[None, :]
    ).astype(bf16)

    def project(pieces):
        ours = jnp.concatenate(pieces, axis=0)
        theirs = swap_core(ours)
        w_here = lax.dynamic_slice_in_dim(weights, core * half_width, half_width, 0)
        w_there = lax.dynamic_slice_in_dim(weights, (1 - core) * half_width, half_width, 0)
        out = jnp.dot(ours, w_here, preferred_element_type=f32) + jnp.dot(
            theirs, w_there, preferred_element_type=f32
        )
        out = out.astype(bf16).reshape(BLOCK, -1, out.shape[1])
        return in_block([out[j] for j in range(BLOCK)])

    from_text = project(in_block([text_states] * BLOCK))
    from_image = project(in_block([owned] * BLOCK))

    mixed = text_states.astype(f32) + jnp.dot(placer, owned, preferred_element_type=f32)
    squares = jnp.sum(mixed * mixed, axis=1)
    squares = squares + swap_core(squares)
    scale = lax.rsqrt(squares / (2 * half_width) + epsilon)[:, None]
    made = [
        (a.astype(f32) + jnp.dot(placer, b, preferred_element_type=f32)) * scale
        for a, b in zip(from_text, from_image)
    ]
    col = jnp.arange(kv_part + q_part) >= kv_part
    soft = jnp.where(col, HD ** (-0.5) * LOG2E, 1.0)[None, :].astype(f32)
    made = jnp.stack([(m * soft).astype(bf16) for m in made])
    qkv = jnp.stack(
        [lax.dynamic_index_in_dim(made, k ^ quarter, 0, keepdims=False) for k in range(BLOCK)]
    )
    clip = jnp.arange(HD, dtype=jnp.int32)[None, :]
    doc_q = (doc_ids[:, None] == clip).astype(bf16)
    doc_k = jnp.where((docs[:, None] != clip) & (clip < CLIPS), FAR, 0.0).astype(bf16)
    return attention(qkv, doc_q, doc_k, kv_local, group)


def solution(mesh):
    in_specs = (
        P(("groups", "seq"), None),
        P(None, "tensor"),
        P("tensor", None),
        P("seq", "tensor"),
        P(("groups", "seq"), "tensor"),
        P("seq", "tensor"),
        P("seq", "tensor"),
        P("seq", "tensor"),
        P(("groups", "seq")),
        P(("groups", "seq")),
    )
    out_specs = P(("groups", "seq"), "tensor")
    return jax.shard_map(body, mesh=mesh, in_specs=in_specs, out_specs=out_specs, check_vma=False)
```

time: 700 us -> 340 us (0.49); the launches traced: 689 us -> 340 us
  waiting for transfers between devices: 403 us -> 178 us
  blocking collectives: 67.1 us -> 0 us
  Pallas kernels: 0 us -> 57.4 us
  matrix products: 89.5 us -> 36.3 us
  other arithmetic: 54.3 us -> 8.64 us
  local copies, waits for them, and re-layouts: 38.2 us -> 11.7 us
  starting transfers between devices: 21.8 us -> 33.8 us
    all_gather x2 -> x1, waiting for transfers between devices: 273 us -> 21.7 us  [body(): weights = lax.all_gather(w_mine, 'seq', axis=0, tiled=True)]
    ppermute x0 -> x17, waiting for transfers between devices: none -> 68.2 us  [the longest x12 67.5 us: in_block(): lax.ppermute(pieces[j], 'groups', swaps[j])]
    pallas_call x0 -> x1, Pallas kernels: none -> 57.4 us  [attention(): pl.pallas_call(functools.partial(attention_kernel, reach, kv_local, group...]
    unnamed x2 -> x0, blocking collectives: 56.6 us -> none
    dot_general x18 -> x11, matrix products: 89.5 us -> 36.3 us  [the longest x1 10.2 us: body(): jnp.dot(activated, vis_down, preferred_element_type=f32).astype(bf16)]
    reduce_scatter x1, waiting for transfers between devices: 83.5 us -> 49 us  [body(): owned = lax.psum_scatter(products, 'seq', scatter_dimension=0, tiled=True)]
    reduce_sum x8 -> x2, other arithmetic: 23.3 us -> 1.29 us  [the longest x1 1.08 us: body(): rank = jnp.sum((dest[None, :] < dest[:, None]).astype(jnp.int32), axis=1)]
    ppermute x0 -> x17, starting transfers between devices: none -> 15.6 us  [the longest x12 14.5 us: in_block(): lax.ppermute(pieces[j], 'groups', swaps[j])]
  transfers between devices with their start and end apart: 5 -> 21, of which waited for: 4 -> 14; matrix products, arithmetic and copies ran while one was open for 6% -> 15% of each run, Pallas kernels for 0% -> 0%
where the time goes in v1:
time: 340 us
  waiting for transfers between devices  178 us (52%)
  Pallas kernels  57.4 us (17%)
  matrix products  36.3 us (11%)
  starting transfers between devices  33.8 us (10%)
  between operations  13.9 us (4%)
  local copies, waits for them, and re-layouts  11.7 us (3%)
  other arithmetic  8.64 us (3%)
    ppermute x12, waiting for transfers between devices, in_block(): lax.ppermute(pieces[j], 'groups', swaps[j])  67.5 us
    pallas_call x1, Pallas kernels, attention(): pl.pallas_call(functools.partial(attention_kernel, reach, kv_local, group...  57.4 us
    reduce_scatter x1, waiting for transfers between devices, body(): owned = lax.psum_scatter(products, 'seq', scatter_dimension=0, tiled=True)  49 us
    all_to_all x1, waiting for transfers between devices, body(): lax.all_to_all(grouped, 'seq', split_axis=1, concat_axis=0, tiled=True)  35.1 us
    all_gather x1, waiting for transfers between devices, body(): weights = lax.all_gather(w_mine, 'seq', axis=0, tiled=True)  21.7 us
    ppermute x12, starting transfers between devices, in_block(): lax.ppermute(pieces[j], 'groups', swaps[j])  14.5 us
    dot_general x1, matrix products, body(): jnp.dot(activated, vis_down, preferred_element_type=f32).astype(bf16)  10.2 us
    dot_general x1, matrix products, body(): jnp.dot(in_order, merge_weight, preferred_element_type=f32).astype(bf16)  9.47 us
  transfers between devices with their start and end apart: 21, of which 14 were waited for; matrix products, arithmetic and copies ran while one was open for 15% of the time, Pallas kernels for 0%

profile of v1, /device:TPU:1604, one launch (start us, length us, event | category | flops | bytes accessed | tf_op | source)
XLA Modules:
  0.0 339.6 jit_solution(16534601662936980058)
XLA Ops:
  6.6 1.1 constant_dynamic-slice_fusion.4
  7.7 0.9 fusion.68
  8.6 0.8 pad_maximum_fusion.2
  10.2 10.2 %convolution_convert_fusion.1 = bf16[384,1152]{1,0:T(8,128)(2,1)S(1)} fusion(bf16[2152,1152]{1,0:T(8,128)(2,1)} %param.12, bf16[1152,2152]{0,1:T(8,128)(2,1)} %param.11, bf16[384,1152]{1,0:T(8,128)(2,1)S(1)} %copy-done.1, f32[384]{0:T(512)S(1)} %add_rsqrt_fusion, f32[384]{0:T(512)S(1)} %broadcast_multiply_fusion), kind=kOutput, calls=%fused_computation.24 | convolution fusion | flops 3817552896 | bytes 11688960 | tf_op jit(solution)/shard_map/dot_general | solution.py:245
  20.4 0.9 constant_dynamic-slice_fusion.5
  21.9 9.4 %all-to-all-start = ((s32[16,1,288]{2,1,0:T(1,128)}), s32[16,1,288]{2,1,0:T(1,128)}, u32[]{:S(2)}, u32[]{:S(2)}) async-start(s32[16,1,288]{2,1,0:T(1,128)} %broadcast_in_dim.26), calls=%async_computation | async-start | bytes 49152 | tf_op jit(solution)/shard_map/all_to_all | solution.py:29
  31.4 1.4 fusion.85
  34.3 1.2 fusion.43
  35.5 3.8 %all-to-all-done = s32[16,1,288]{2,1,0:T(1,128)} async-done(((s32[16,1,288]{2,1,0:T(1,128)}), s32[16,1,288]{2,1,0:T(1,128)}, u32[]{:S(2)}, u32[]{:S(2)}) %all-to-all-start) | async-done | bytes 18464 | tf_op jit(solution)/shard_map/all_to_all | solution.py:29
  39.3 8.7 %all-to-all-start.1 = ((bf16[48,16,288]{2,0,1:T(8,128)(2,1)}), bf16[48,16,288]{2,0,1:T(8,128)(2,1)S(1)}, u32[]{:S(2)}, u32[]{:S(2)}) async-start(bf16[48,16,288]{2,0,1:T(8,128)(2,1)} %fusion.43), calls=%async_computation.1 | async-start | bytes 1179648 | tf_op jit(solution)/shard_map/all_to_all | solution.py:255
  48.1 0.7 copy.25
  49.1 35.1 %all-to-all-done.1 = bf16[48,16,288]{2,0,1:T(8,128)(2,1)S(1)} async-done(((bf16[48,16,288]{2,0,1:T(8,128)(2,1)}), bf16[48,16,288]{2,0,1:T(8,128)(2,1)S(1)}, u32[]{:S(2)}, u32[]{:S(2)}) %all-to-all-start.1) | async-done | bytes 442400 | tf_op jit(solution)/shard_map/all_to_all | solution.py:255
  84.7 1.1 convert_reduce_fusion
  85.8 0.7 collective-permute-done.4
  86.8 9.5 %convolution_convert_fusion = bf16[1536,2560]{1,0:T(8,128)(2,1)} fusion(bf16[288,2560]{1,0:T(8,128)(2,1)S(1)} %copy-done, s32[1536]{0:T(1024)S(1)} %convert_reduce_fusion, bf16[768,288]{1,0:T(8,128)(2,1)S(1)} %copy.17, bf16[768,288]{1,0:T(8,128)(2,1)S(1)} %bitcast.26), kind=kOutput, calls=%fused_computation | convolution fusion | flops 3632381952 | bytes 10229760 | tf_op jit(solution)/shard_map/dot_general | solution.py:266
  96.2 21.7 %all-gather.2.cloned.1.call-done = bf16[5120,640]{1,0:T(8,128)(2,1)} async-done(((bf16[320,640]{1,0:T(8,128)(2,1)}), bf16[5120,640]{1,0:T(8,128)(2,1)}) %all-gather.2.cloned.1.call-update) | async-done | bytes 6553616 | tf_op jit(solution)/shard_map/all_gather | solution.py:234
  118.0 1.6 collective-permute-start
  119.6 1.5 collective-permute-start.1
  121.6 1.0 constant_dynamic-update-slice_fusion.3
  122.6 19.2 %collective-permute-done = bf16[192,2560]{1,0:T(8,128)(2,1)S(1)} collective-permute-done((bf16[192,2560]{1,0:T(8,128)(2,1)S(1)}, bf16[192,2560]{1,0:T(8,128)(2,1)S(1)}, u32[]{:S(2)}, u32[]{:S(2)}) %collective-permute-start) | collective-permute-done | bytes 983072 | tf_op jit(solution)/shard_map/ppermute | solution.py:223
  141.8 1.0 constant_dynamic-update-slice_fusion.2
  142.9 1.4 collective-permute-done.1
  144.2 1.0 constant_dynamic-update-slice_fusion.1
  145.2 18.5 %collective-permute-done.2 = bf16[192,2560]{1,0:T(8,128)(2,1)S(1)} collective-permute-done((bf16[192,2560]{1,0:T(8,128)(2,1)S(1)}, bf16[192,2560]{1,0:T(8,128)(2,1)S(1)}, u32[]{:S(2)}, u32[]{:S(2)}) %collective-permute-start.2) | collective-permute-done | bytes 983072 | tf_op jit(solution)/shard_map/ppermute | solution.py:223
  163.7 1.0 constant_dynamic-update-slice_fusion
  165.2 1.4 select_convert_fusion.doc_k_ref
  166.6 49.0 %reduce-scatter.2.cloned.1.call-done = bf16[96,2560]{1,0:T(8,128)(2,1)} async-done(((bf16[1536,2560]{1,0:T(8,128)(2,1)}), bf16[96,2560]{1,0:T(8,128)(2,1)}) %reduce-scatter.2.cloned.1.call-update) | async-done | bytes 491536 | tf_op jit(solution)/shard_map/reduce_scatter | solution.py:268
  215.6 1.5 collective-permute-start.6
  217.1 1.5 collective-permute-start.7
  218.6 1.1 constant_dynamic-update-slice_fusion.8
  219.7 0.6 collective-permute-start.8
  220.3 8.7 %collective-permute-done.6 = bf16[96,2560]{1,0:T(8,128)(2,1)S(1)} collective-permute-done((bf16[96,2560]{1,0:T(8,128)(2,1)}, bf16[96,2560]{1,0:T(8,128)(2,1)S(1)}, u32[]{:S(2)}, u32[]{:S(2)}) %collective-permute-start.6) | collective-permute-done | bytes 491552 | tf_op jit(solution)/shard_map/ppermute | solution.py:223
  229.1 2.4 collective-permute-done.7
  231.5 9.0 %collective-permute-done.8 = bf16[96,2560]{1,0:T(8,128)(2,1)S(1)} collective-permute-done((bf16[96,2560]{1,0:T(8,128)(2,1)}, bf16[96,2560]{1,0:T(8,128)(2,1)S(1)}, u32[]{:S(2)}, u32[]{:S(2)}) %collective-permute-start.8) | collective-permute-done | bytes 491552 | tf_op jit(solution)/shard_map/ppermute | solution.py:223
  240.9 6.5 %fusion.13 = f32[768,640]{1,0:T(8,128)S(1)} fusion(bf16[768,2560]{1,0:T(8,128)(2,1)} %collective-permute-done.5, bf16[5120,640]{1,0:T(8,128)(2,1)} %all-gather.2.cloned.1.call-done, s32[]{:T(128)S(6)} %select_n.87), kind=kOutput, calls=%fused_computation.18 | convolution fusion | flops 2516582400 | bytes 9175044 | tf_op jit(solution)/shard_map/dot_general | solution.py:284
  247.4 5.4 %add_convert_fusion = bf16[768,640]{1,0:T(8,128)(2,1)S(1)} fusion(f32[768,640]{1,0:T(8,128)S(1)} %fusion.13, bf16[768,2560]{1,0:T(8,128)(2,1)} %constant_dynamic-update-slice_fusion, bf16[5120,640]{1,0:T(8,128)(2,1)S(1)} %bitcast.30, s32[]{:T(128)S(6)} %select_n.86), kind=kOutput, calls=%fused_computation.30 | convolution fusion | flops 2517565440 | bytes 10158084 | tf_op jit(solution)/shard_map/dot_general | solution.py:284
  253.8 1.6 collective-permute-start.11
  255.4 1.5 collective-permute-start.13
  257.4 1.7 fusion.11
  259.1 1.7 fusion.36
  260.9 1.6 collective-permute-start.12
  262.5 1.5 collective-permute-start.14
  264.2 0.6 collective-permute-start.16
  264.8 6.0 %collective-permute-done.12 = bf16[96,640]{1,0:T(8,128)(2,1)S(1)} collective-permute-done((bf16[96,640]{1,0:T(8,128)(2,1)S(1)}, bf16[96,640]{1,0:T(8,128)(2,1)S(1)}, u32[]{:S(2)}, u32[]{:S(2)}) %collective-permute-start.12) | collective-permute-done | bytes 122912 | tf_op jit(solution)/shard_map/ppermute | solution.py:223
  271.1 1.1 collective-permute-done.14
  272.4 1.4 collective-permute-done.16
  274.4 57.4 %attend.1 = bf16[192,2048]{1,0:T(8,128)(2,1)S(1)} custom-call(bf16[4,192,640]{2,1,0:T(8,128)(2,1)S(1)} %pad_maximum_fusion.1.qkv_ref, bf16[192,128]{1,0:T(8,128)(2,1)S(1)} %fusion.67.doc_q_ref, bf16[3072,128]{1,0:T(8,128)(2,1)S(1)} %select_convert_fusion.doc_k_ref), custom_call_target="tpu_custom_call" | custom-call | flops 2717908992 | bytes 3932160 | tf_op jit(solution)/shard_map/attend/pallas_call | solution.py:175
  331.9 0.9 copy.35
  (84 shorter events, 8.3 us)
Async XLA Ops:
  6.5 80.2 %copy-start = (bf16[288,2560]{1,0:T(8,128)(2,1)S(1)}, bf16[288,2560]{1,0:T(8,128)(2,1)}, u32[]{:S(2)}) copy-start(bf16[288,2560]{1,0:T(8,128)(2,1)} %param.13) | copy-start | bytes 4423684
  6.6 3.0 copy-start.1
  6.6 111.4 %all-gather.2.cloned.1.call-start = ((), (), s32[]{:S(2)}) async-start(), calls=%async_computation.3 | async-start | bytes 6963200 | tf_op jit(solution)/shard_map/all_gather | solution.py:234
  10.1 11.1 %copy-start.5 = (s32[192]{0:T(256)S(1)}, s32[192]{0:T(256)}, u32[]{:S(2)}) copy-start(s32[192]{0:T(256)} %param.19) | copy-start | bytes 2308
  10.1 11.1 %copy-start.6 = (s32[96]{0:T(128)S(1)}, s32[96]{0:T(128)}, u32[]{:S(2)}) copy-start(s32[96]{0:T(128)} %param.18) | copy-start | bytes 1156
  20.3 11.0 %copy-start.3 = (bf16[384,1152]{1,0:T(8,128)(2,1)}, bf16[384,1152]{1,0:T(8,128)(2,1)S(1)}, u32[]{:S(2)}) copy-start(bf16[384,1152]{1,0:T(8,128)(2,1)S(1)} %convolution_convert_fusion.1) | copy-start | bytes 2654212
  21.2 10.1 %collective-permute-start.3 = (bf16[192,1152]{1,0:T(8,128)(2,1)}, bf16[192,1152]{1,0:T(8,128)(2,1)}, u32[]{:S(2)}, u32[]{:S(2)}) collective-permute-start(bf16[192,1152]{1,0:T(8,128)(2,1)} %constant_dynamic-slice_fusion.5), channel_id=1, source_target_pairs={{0,1},{1,0},{2,3},{3,2},{4,5},{5,4},{6,7},{7,6},{8,9},{9,8},{10,11... | collective-permute-start | bytes 1327112 | tf_op jit(solution)/shard_map/ppermute | solution.py:35
  21.9 17.3 %all-to-all-start = ((s32[16,1,288]{2,1,0:T(1,128)}), s32[16,1,288]{2,1,0:T(1,128)}, u32[]{:S(2)}, u32[]{:S(2)}) async-start(s32[16,1,288]{2,1,0:T(1,128)} %broadcast_in_dim.26), calls=%async_computation | async-start | bytes 49152 | tf_op jit(solution)/shard_map/all_to_all | solution.py:29
  39.3 44.9 %all-to-all-start.1 = ((bf16[48,16,288]{2,0,1:T(8,128)(2,1)}), bf16[48,16,288]{2,0,1:T(8,128)(2,1)S(1)}, u32[]{:S(2)}, u32[]{:S(2)}) async-start(bf16[48,16,288]{2,0,1:T(8,128)(2,1)} %fusion.43), calls=%async_computation.1 | async-start | bytes 1179648 | tf_op jit(solution)/shard_map/all_to_all | solution.py:255
  48.0 167.6 %reduce-scatter.2.cloned.1.call-start = ((), (), s32[]{:S(2)}) async-start(), calls=%async_computation.4 | async-start | bytes 8355840 | tf_op jit(solution)/shard_map/reduce_scatter | solution.py:268
  84.4 2.1 collective-permute-start.4
  96.2 21.7 %copy-start.2 = (bf16[192,2560]{1,0:T(8,128)(2,1)S(1)}, bf16[192,2560]{1,0:T(8,128)(2,1)}, u32[]{:S(2)}) copy-start(bf16[192,2560]{1,0:T(8,128)(2,1)} %param.14) | copy-start | bytes 2949124
  118.0 23.8 %collective-permute-start = (bf16[192,2560]{1,0:T(8,128)(2,1)S(1)}, bf16[192,2560]{1,0:T(8,128)(2,1)S(1)}, u32[]{:S(2)}, u32[]{:S(2)}) collective-permute-start(bf16[192,2560]{1,0:T(8,128)(2,1)S(1)} %copy-done.2), channel_id=1, source_target_pairs={{0,32},{32,0},{64,96},{96,64},{1,33},{33,1},{65,97},{97,65},{2,34}... | collective-permute-start | bytes 2949128 | tf_op jit(solution)/shard_map/ppermute | solution.py:223
  119.6 24.6 %collective-permute-start.1 = (bf16[192,2560]{1,0:T(8,128)(2,1)S(1)}, bf16[192,2560]{1,0:T(8,128)(2,1)S(1)}, u32[]{:S(2)}, u32[]{:S(2)}) collective-permute-start(bf16[192,2560]{1,0:T(8,128)(2,1)S(1)} %copy-done.2), channel_id=1, source_target_pairs={{0,64},{32,96},{64,0},{96,32},{1,65},{33,97},{65,1},{97,33},{2,66}... | collective-permute-start | bytes 2949128 | tf_op jit(solution)/shard_map/ppermute | solution.py:223
  121.1 42.6 %collective-permute-start.2 = (bf16[192,2560]{1,0:T(8,128)(2,1)S(1)}, bf16[192,2560]{1,0:T(8,128)(2,1)S(1)}, u32[]{:S(2)}, u32[]{:S(2)}) collective-permute-start(bf16[192,2560]{1,0:T(8,128)(2,1)S(1)} %copy-done.2), channel_id=1, source_target_pairs={{0,96},{32,64},{64,32},{96,0},{1,97},{33,65},{65,33},{97,1},{2,98}... | collective-permute-start | bytes 2949128 | tf_op jit(solution)/shard_map/ppermute | solution.py:223
  164.7 76.1 %collective-permute-start.5 = (bf16[768,2560]{1,0:T(8,128)(2,1)}, bf16[768,2560]{1,0:T(8,128)(2,1)}, u32[]{:S(2)}, u32[]{:S(2)}) collective-permute-start(bf16[768,2560]{1,0:T(8,128)(2,1)} %constant_dynamic-update-slice_fusion), channel_id=1, source_target_pairs={{0,1},{1,0},{2,3},{3,2},{4,5},{5,4},{6,7},{7,6},{8,9},{9,8},{10,11... | collective-permute-start | bytes 11796488 | tf_op jit(solution)/shard_map/ppermute | solution.py:35
  215.6 13.4 %collective-permute-start.6 = (bf16[96,2560]{1,0:T(8,128)(2,1)}, bf16[96,2560]{1,0:T(8,128)(2,1)S(1)}, u32[]{:S(2)}, u32[]{:S(2)}) collective-permute-start(bf16[96,2560]{1,0:T(8,128)(2,1)} %reduce-scatter.2.cloned.1.call-done), channel_id=1, source_target_pairs={{0,32},{32,0},{64,96},{96,64},{1,33},{33,1},{65,97},{97,65},{2,34}... | collective-permute-start | bytes 1474568 | tf_op jit(solution)/shard_map/ppermute | solution.py:223
  217.1 14.3 %collective-permute-start.7 = (bf16[96,2560]{1,0:T(8,128)(2,1)}, bf16[96,2560]{1,0:T(8,128)(2,1)S(1)}, u32[]{:S(2)}, u32[]{:S(2)}) collective-permute-start(bf16[96,2560]{1,0:T(8,128)(2,1)} %reduce-scatter.2.cloned.1.call-done), channel_id=1, source_target_pairs={{0,64},{32,96},{64,0},{96,32},{1,65},{33,97},{65,1},{97,33},{2,66}... | collective-permute-start | bytes 1474568 | tf_op jit(solution)/shard_map/ppermute | solution.py:223
  219.7 20.8 %collective-permute-start.8 = (bf16[96,2560]{1,0:T(8,128)(2,1)}, bf16[96,2560]{1,0:T(8,128)(2,1)S(1)}, u32[]{:S(2)}, u32[]{:S(2)}) collective-permute-start(bf16[96,2560]{1,0:T(8,128)(2,1)} %reduce-scatter.2.cloned.1.call-done), channel_id=1, source_target_pairs={{0,96},{32,64},{64,32},{96,0},{1,97},{33,65},{65,33},{97,1},{2,98}... | collective-permute-start | bytes 1474568 | tf_op jit(solution)/shard_map/ppermute | solution.py:223
  240.4 7.0 %slice-start = ((s8[6553600]{0:T(1024)(128)(4,1)}), s8[4194304]{0:T(1024)(128)(4,1)S(1)}, s32[]{:S(2)}) async-start(s8[6553600]{0:T(1024)(128)(4,1)} %bitcast.29), calls=%async_computation.5 | async-start | bytes 8388608
  240.5 6.9 %slice-start.1 = ((s8[6553600]{0:T(1024)(128)(4,1)}), s8[2359296]{0:T(1024)(128)(4,1)S(1)}, s32[]{:S(2)}) async-start(s8[6553600]{0:T(1024)(128)(4,1)} %bitcast.29), calls=%async_computation.6 | async-start | bytes 4718592
  240.5 16.9 %collective-permute-start.9 = (bf16[384,2560]{1,0:T(8,128)(2,1)S(1)}, bf16[384,2560]{1,0:T(8,128)(2,1)S(1)}, u32[]{:S(2)}, u32[]{:S(2)}) collective-permute-start(bf16[384,2560]{1,0:T(8,128)(2,1)S(1)} %constant_dynamic-update-slice_fusion.5), channel_id=1, source_target_pairs={{0,1},{1,0},{2,3},{3,2},{4,5},{5,4},{6,7},{7,6},{8,9},{9,8},{10,11... | collective-permute-start | bytes 5898248 | tf_op jit(solution)/shard_map/ppermute | solution.py:35
  247.4 5.4 %copy-start.4 = (bf16[96,2560]{1,0:T(8,128)(2,1)S(1)}, bf16[96,2560]{1,0:T(8,128)(2,1)}, u32[]{:S(2)}) copy-start(bf16[96,2560]{1,0:T(8,128)(2,1)} %reduce-scatter.2.cloned.1.call-done) | copy-start | bytes 1474564
  253.3 4.1 %collective-permute-start.10 = (f32[192]{0:T(256)S(1)}, f32[192]{0:T(256)S(1)}, u32[]{:S(2)}, u32[]{:S(2)}) collective-permute-start(f32[192]{0:T(256)S(1)} %fusion.32), channel_id=1, source_target_pairs={{0,1},{1,0},{2,3},{3,2},{4,5},{5,4},{6,7},{7,6},{8,9},{9,8},{10,11... | collective-permute-start | bytes 2312 | tf_op jit(solution)/shard_map/ppermute | solution.py:35
  253.8 10.4 %collective-permute-start.11 = (bf16[192,640]{1,0:T(8,128)(2,1)S(1)}, bf16[192,640]{1,0:T(8,128)(2,1)S(1)}, u32[]{:S(2)}, u32[]{:S(2)}) collective-permute-start(bf16[192,640]{1,0:T(8,128)(2,1)S(1)} %get-tuple-element.15), channel_id=1, source_target_pairs={{0,32},{32,0},{64,96},{96,64},{1,33},{33,1},{65,97},{97,65},{2,34}... | collective-permute-start | bytes 737288 | tf_op jit(solution)/shard_map/ppermute | solution.py:223
  255.4 15.7 %collective-permute-start.13 = (bf16[192,640]{1,0:T(8,128)(2,1)S(1)}, bf16[192,640]{1,0:T(8,128)(2,1)S(1)}, u32[]{:S(2)}, u32[]{:S(2)}) collective-permute-start(bf16[192,640]{1,0:T(8,128)(2,1)S(1)} %get-tuple-element.17), channel_id=1, source_target_pairs={{0,64},{32,96},{64,0},{96,32},{1,65},{33,97},{65,1},{97,33},{2,66}... | collective-permute-start | bytes 737288 | tf_op jit(solution)/shard_map/ppermute | solution.py:223
  256.9 15.5 %collective-permute-start.15 = (bf16[192,640]{1,0:T(8,128)(2,1)S(1)}, bf16[192,640]{1,0:T(8,128)(2,1)S(1)}, u32[]{:S(2)}, u32[]{:S(2)}) collective-permute-start(bf16[192,640]{1,0:T(8,128)(2,1)S(1)} %get-tuple-element.16), channel_id=1, source_target_pairs={{0,96},{32,64},{64,32},{96,0},{1,97},{33,65},{65,33},{97,1},{2,98}... | collective-permute-start | bytes 737288 | tf_op jit(solution)/shard_map/ppermute | solution.py:223
  260.9 10.0 %collective-permute-start.12 = (bf16[96,640]{1,0:T(8,128)(2,1)S(1)}, bf16[96,640]{1,0:T(8,128)(2,1)S(1)}, u32[]{:S(2)}, u32[]{:S(2)}) collective-permute-start(bf16[96,640]{1,0:T(8,128)(2,1)S(1)} %get-tuple-element.18), channel_id=1, source_target_pairs={{0,32},{32,0},{64,96},{96,64},{1,33},{33,1},{65,97},{97,65},{2,34}... | collective-permute-start | bytes 368648 | tf_op jit(solution)/shard_map/ppermute | solution.py:223
  262.5 9.7 %collective-permute-start.14 = (bf16[96,640]{1,0:T(8,128)(2,1)S(1)}, bf16[96,640]{1,0:T(8,128)(2,1)S(1)}, u32[]{:S(2)}, u32[]{:S(2)}) collective-permute-start(bf16[96,640]{1,0:T(8,128)(2,1)S(1)} %get-tuple-element.20), channel_id=1, source_target_pairs={{0,64},{32,96},{64,0},{96,32},{1,65},{33,97},{65,1},{97,33},{2,66}... | collective-permute-start | bytes 368648 | tf_op jit(solution)/shard_map/ppermute | solution.py:223
  264.2 9.6 %collective-permute-start.16 = (bf16[96,640]{1,0:T(8,128)(2,1)S(1)}, bf16[96,640]{1,0:T(8,128)(2,1)S(1)}, u32[]{:S(2)}, u32[]{:S(2)}) collective-permute-start(bf16[96,640]{1,0:T(8,128)(2,1)S(1)} %get-tuple-element.19), channel_id=1, source_target_pairs={{0,96},{32,64},{64,32},{96,0},{1,97},{33,65},{65,33},{97,1},{2,98}... | collective-permute-start | bytes 368648 | tf_op jit(solution)/shard_map/ppermute | solution.py:223
Sparse Core Ops, SparseCore 0:
  9.6 108.2 all-gather.1
  120.4 95.2 reduce-scatter.1

commit v2 on v1

--- a/solution.py
+++ b/solution.py
@@ -55,7 +55,8 @@
 ):
     me = lax.axis_index("seq")
     count = lax.axis_size("seq")
-    rows = qkv_ref.shape[1]
+    rows = qkv_ref.shape[0]
+    width = qkv_ref.shape[1] // BLOCK
     MESH = pl.DeviceIdType.MESH
 
     barrier = pltpu.get_barrier_semaphore()
@@ -68,88 +69,94 @@
     def _():
         pl.semaphore_signal(barrier, inc=1, device_id={"seq": me + 1}, device_id_type=MESH)
 
-    for i in range(2 * kv_local):
-        kv_buf[0, :, i * HD : (i + 1) * HD] = qkv_ref[i, :, :HD]
+    wide = math.isqrt(lax.axis_size("groups"))
+    index = lax.axis_index("groups")
+    own_row, own_col = lax.rem(index // wide, 2), lax.rem(index, 2)
+
+    def columns_of(k, at):
+        row, col = k // 2, k % 2
+        j = 2 * (row + own_row - 2 * row * own_row) + (col + own_col - 2 * col * own_col)
+        return qkv_ref[:, pl.ds(pl.multiple_of(j * width + at * HD, HD), HD)]
+
+    for g in range(kv_local):
+        kv_buf[0, g, :, :HD] = columns_of(g, 0)
+        kv_buf[0, g, :, HD:] = columns_of(kv_local + g, 0)
 
     pl.semaphore_wait(barrier, jnp.minimum(me, 1) + jnp.minimum(count - 1 - me, 1))
 
-    half = kv_local * HD
-
-    def pass_on(slot, part):
-        cols = pl.ds(part * half, half)
+    piece = rows // 2
+
+    def pass_on(slot, g, part):
+        spot = pl.ds(part * piece, piece)
         return pltpu.make_async_remote_copy(
-            src_ref=kv_buf.at[slot, :, cols],
-            dst_ref=kv_buf.at[slot + 1, :, cols],
-            send_sem=send_sem.at[slot, part],
-            recv_sem=recv_sem.at[slot, part],
+            src_ref=kv_buf.at[slot, g, spot, :],
+            dst_ref=kv_buf.at[slot + 1, g, spot, :],
+            send_sem=send_sem.at[slot, g, part],
+            recv_sem=recv_sem.at[slot, g, part],
             device_id={"seq": me + 1},
             device_id_type=MESH,
         )
 
     @pl.when(me < count - 1)
     def _():
-        pass_on(0, 0).start()
-        pass_on(0, 1).start()
+        for g in range(kv_local):
+            for part in range(2):
+                pass_on(0, g, part).start()
 
     doc_q = doc_q_ref[...]
-    per = BLOCK
     for h in range(kv_local * group):
         g, i = divmod(h, group)
         spot = pl.ds(i * rows, rows)
-        k, j = divmod(h, per)
-        q_buf[g, spot, :HD] = qkv_ref[k, :, (1 + j) * HD : (2 + j) * HD]
+        k, j = divmod(h, BLOCK)
+        q_buf[g, spot, :HD] = columns_of(k, 1 + j)
         q_buf[g, spot, HD:] = doc_q
     chunk = 2 * rows
 
-    def visit(slot, start):
+    def visit(slot, g, start, own):
         doc_k = doc_k_ref[pl.ds(pl.multiple_of(start, rows), rows), :]
         ones = jnp.ones((rows, HD), jnp.bfloat16)
-
-        @pl.loop(0, kv_local)
-        def _(g):
-            at = pl.multiple_of(g * HD, HD)
-            keys = jnp.concatenate([kv_buf[slot, :, pl.ds(at, HD)], doc_k], axis=1)
-            vals = jnp.concatenate([kv_buf[slot, :, pl.ds(half + at, HD)], ones], axis=1)
-            for b in range(group * rows // chunk):
-                spot = pl.ds(b * chunk, chunk)
-                s = lax.dot_general(
-                    q_buf[g, spot, :], keys, (((1,), (1,)), ((), ())),
-                    preferred_element_type=jnp.float32,
+        keys = jnp.concatenate([kv_buf[slot, g, :, :HD], doc_k], axis=1)
+        vals = jnp.concatenate([kv_buf[slot, g, :, HD:], ones], axis=1)
+        for b in range(group * rows // chunk):
+            spot = pl.ds(b * chunk, chunk)
+            s = lax.dot_general(
+                q_buf[g, spot, :], keys, (((1,), (1,)), ((), ())),
+                preferred_element_type=jnp.float32,
+            )
+            if own:
+                token = lax.rem(lax.broadcasted_iota(jnp.int32, s.shape, 0), jnp.int32(rows))
+                other = lax.broadcasted_iota(jnp.int32, s.shape, 1)
+                s = jnp.where(other <= token, s, FAR)
+                high = jnp.max(s, axis=1, keepdims=True)
+                raw = jnp.exp2(s - high).astype(jnp.bfloat16)
+                total[g, spot, :] = jnp.dot(raw, vals, preferred_element_type=jnp.float32)
+            else:
+                before = top[g, spot, :]
+                high = jnp.maximum(before, jnp.max(s, axis=1, keepdims=True))
+                raw = jnp.exp2(s - high).astype(jnp.bfloat16)
+                total[g, spot, :] = total[g, spot, :] * jnp.exp2(before - high) + jnp.dot(
+                    raw, vals, preferred_element_type=jnp.float32
                 )
-                first = isinstance(slot, int)
-                if first:
-                    token = lax.rem(
-                        lax.broadcasted_iota(jnp.int32, s.shape, 0), jnp.int32(rows)
-                    )
-                    other = lax.broadcasted_iota(jnp.int32, s.shape, 1)
-                    s = jnp.where(other <= token, s, FAR)
-                    high = jnp.max(s, axis=1, keepdims=True)
-                    raw = jnp.exp2(s - high).astype(jnp.bfloat16)
-                    total[g, spot, :] = jnp.dot(raw, vals, preferred_element_type=jnp.float32)
-                    top[g, spot, :] = high
-                else:
-                    before = top[g, spot, :]
-                    high = jnp.maximum(before, jnp.max(s, axis=1, keepdims=True))
-                    raw = jnp.exp2(s - high).astype(jnp.bfloat16)
-                    total[g, spot, :] = total[g, spot, :] * jnp.exp2(before - high) + jnp.dot(
-                        raw, vals, preferred_element_type=jnp.float32
-                    )
-                    top[g, spot, :] = high
-
-    visit(0, me * rows)
+            top[g, spot, :] = high
+
+    @pl.loop(0, kv_local)
+    def _(g):
+        visit(0, g, me * rows, True)
 
     @pl.loop(1, reach + 1)
     def _(slot):
         @pl.when(slot <= me)
         def _():
-            for part in range(2):
-                pass_on(slot - 1, part).wait_recv()
-
-                @pl.when((slot < reach) & (me < count - 1))
-                def _():
-                    pass_on(slot, part).start()
-
-            visit(slot, (me - slot) * rows)
+            @pl.loop(0, kv_local)
+            def _(g):
+                for part in range(2):
+                    pass_on(slot - 1, g, part).wait_recv()
+
+                    @pl.when((slot < reach) & (me < count - 1))
+                    def _():
+                        pass_on(slot, g, part).start()
+
+                visit(slot, g, (me - slot) * rows, False)
 
     for h in range(kv_local * group):
         g, i = divmod(h, group)
@@ -162,12 +169,13 @@
     def _(slot):
         @pl.when((slot <= me) & (me < count - 1))
         def _():
-            for part in range(2):
-                pass_on(slot, part).wait_send()
+            for g in range(kv_local):
+                for part in range(2):
+                    pass_on(slot, g, part).wait_send()
 
 
 def attention(qkv, doc_q, doc_k, kv_local, group):
-    rows = qkv.shape[1]
+    rows = qkv.shape[0]
     reach = -(-(REACH - 1) // rows)
     vmem = pl.BlockSpec(memory_space=pltpu.VMEM)
     heads = kv_local * group
@@ -178,12 +186,12 @@
         in_specs=[vmem] * 3,
         out_specs=vmem,
         scratch_shapes=[
-            pltpu.VMEM((reach + 1, rows, 2 * kv_local * HD), jnp.bfloat16),
+            pltpu.VMEM((reach + 1, kv_local, rows, 2 * HD), jnp.bfloat16),
             pltpu.VMEM((kv_local, group * rows, 2 * HD), jnp.bfloat16),
             pltpu.VMEM((kv_local, group * rows, 1), jnp.float32),
             pltpu.VMEM((kv_local, group * rows, 2 * HD), jnp.float32),
-            pltpu.SemaphoreType.DMA((reach, 2)),
-            pltpu.SemaphoreType.DMA((reach, 2)),
+            pltpu.SemaphoreType.DMA((reach, kv_local, 2)),
+            pltpu.SemaphoreType.DMA((reach, kv_local, 2)),
         ],
         compiler_params=pltpu.CompilerParams(
             collective_id=0, has_side_effects=True, vmem_limit_bytes=48 << 20
@@ -231,7 +239,9 @@
         ],
         axis=1,
     )
-    weights = lax.all_gather(w_mine, "seq", axis=0, tiled=True)
+    late = HD
+    early = kv_part + q_part - late
+    weights = lax.all_gather(w_mine[:, :early], "seq", axis=0, tiled=True)
 
     ints = everyones(jnp.concatenate([dest_rows, doc_ids]), "seq")
     merged_rows = dest_rows.shape[0]
@@ -276,34 +286,59 @@
         jnp.arange(text_rows, dtype=jnp.int32)[:, None] == landing[None, :]
     ).astype(bf16)
 
-    def project(pieces):
+    def both_halves(pieces):
         ours = jnp.concatenate(pieces, axis=0)
-        theirs = swap_core(ours)
-        w_here = lax.dynamic_slice_in_dim(weights, core * half_width, half_width, 0)
-        w_there = lax.dynamic_slice_in_dim(weights, (1 - core) * half_width, half_width, 0)
+        return ours, swap_core(ours)
+
+    def project(rows, w):
+        ours, theirs = rows
+        w_here = lax.dynamic_slice_in_dim(w, core * half_width, half_width, 0)
+        w_there = lax.dynamic_slice_in_dim(w, (1 - core) * half_width, half_width, 0)
         out = jnp.dot(ours, w_here, preferred_element_type=f32) + jnp.dot(
             theirs, w_there, preferred_element_type=f32
         )
-        out = out.astype(bf16).reshape(BLOCK, -1, out.shape[1])
-        return in_block([out[j] for j in range(BLOCK)])
-
-    from_text = project(in_block([text_states] * BLOCK))
-    from_image = project(in_block([owned] * BLOCK))
+        return out.astype(bf16).reshape(BLOCK, -1, out.shape[1])
+
+    text_in = both_halves(in_block([text_states] * BLOCK))
+    text_out = project(text_in, weights)
+    text_out = in_block([text_out[j] for j in range(BLOCK)])
+    owned, text_out = lax.optimization_barrier((owned, text_out))
+    w_late, owned = lax.optimization_barrier((w_mine[:, early:], owned))
+    weights_late = lax.all_gather(w_late, "seq", axis=0, tiled=True)
+    image_in = both_halves(in_block([owned] * BLOCK))
+    image_out = project(image_in, weights)
+    image_late = project(image_in, weights_late)
+    text_late = project(text_in, weights_late)
+    cut = text_rows // 2
+    back = jnp.concatenate(
+        [image_out, image_late, text_late[:, :cut], text_late[:, cut:]], axis=2
+    )
+    back = in_block([back[j] for j in range(BLOCK)])
 
     mixed = text_states.astype(f32) + jnp.dot(placer, owned, preferred_element_type=f32)
     squares = jnp.sum(mixed * mixed, axis=1)
     squares = squares + swap_core(squares)
     scale = lax.rsqrt(squares / (2 * half_width) + epsilon)[:, None]
-    made = [
-        (a.astype(f32) + jnp.dot(placer, b, preferred_element_type=f32)) * scale
-        for a, b in zip(from_text, from_image)
-    ]
-    col = jnp.arange(kv_part + q_part) >= kv_part
-    soft = jnp.where(col, HD ** (-0.5) * LOG2E, 1.0)[None, :].astype(f32)
-    made = jnp.stack([(m * soft).astype(bf16) for m in made])
-    qkv = jnp.stack(
-        [lax.dynamic_index_in_dim(made, k ^ quarter, 0, keepdims=False) for k in range(BLOCK)]
-    )
+    width = early + late
+    from_image = jnp.concatenate([p[:, :width] for p in back], axis=1)
+    from_text = jnp.concatenate(
+        [
+            x
+            for t, p in zip(text_out, back)
+            for x in (
+                t,
+                jnp.concatenate([p[:, width : width + late], p[:, width + late :]], axis=0),
+            )
+        ],
+        axis=1,
+    )
+    is_query = jnp.arange(BLOCK * width) % width >= kv_part
+    soft = jnp.where(is_query, HD ** (-0.5) * LOG2E, 1.0)[None, :].astype(f32)
+    qkv = (
+        (from_text.astype(f32) + jnp.dot(placer, from_image, preferred_element_type=f32))
+        * scale
+        * soft
+    ).astype(bf16)
     clip = jnp.arange(HD, dtype=jnp.int32)[None, :]
     doc_q = (doc_ids[:, None] == clip).astype(bf16)
     doc_k = jnp.where((docs[:, None] != clip) & (clip < CLIPS), FAR, 0.0).astype(bf16)

time: 340 us -> 362 us (1.065)
  matrix products: 36.3 us -> 47.8 us
  local copies, waits for them, and re-layouts: 11.7 us -> 19.2 us
  Pallas kernels: 57.4 us -> 52 us
    all_gather x1 -> x2, waiting for transfers between devices: 21.7 us -> 46 us  [the longest x1 35.7 us: body(): weights_late = lax.all_gather(w_late, 'seq', axis=0, tiled=True)]
    reduce_scatter x1, waiting for transfers between devices: 49 us -> 26 us  [body(): owned = lax.psum_scatter(products, 'seq', scatter_dimension=0, tiled=True)]
    ppermute x5, waiting for transfers between devices: 0.67 us -> 7.22 us  [swap_core(): return lax.ppermute(x, 'tensor', [(0, 1), (1, 0)])]
    dot_general x2 -> x4, matrix products: 8.21 us -> 14.5 us  [project(): jnp.dot(theirs, w_there, preferred_element_type=f32)]
    dot_general x2 -> x4, matrix products: 7.09 us -> 12.7 us  [project(): jnp.dot(ours, w_here, preferred_element_type=f32)]
    pallas_call x1, Pallas kernels: 57.4 us -> 52 us  [attention(): pl.pallas_call(functools.partial(attention_kernel, reach, kv_local, group...]
    unnamed x27 -> x51, local copies, waits for them, and re-layouts: 5.89 us -> 9.29 us
  transfers between devices with their start and end apart: 21 -> 22, of which waited for: 14 -> 20; matrix products, arithmetic and copies ran while one was open for 15% -> 17% of each run, Pallas kernels for 0% -> 0%
where the time goes in v2:
time: 362 us; the launch traced here: 359 us
  waiting for transfers between devices  181 us (50%)
  Pallas kernels  52 us (14%)
  matrix products  47.8 us (13%)
  starting transfers between devices  35.3 us (10%)
  local copies, waits for them, and re-layouts  19.2 us (5%)
  between operations  13.7 us (4%)
  other arithmetic  9.69 us (3%)
    ppermute x12, waiting for transfers between devices, in_block(): lax.ppermute(pieces[j], 'groups', swaps[j])  64.4 us
    pallas_call x1, Pallas kernels, attention(): pl.pallas_call(functools.partial(attention_kernel, reach, kv_local, group...  52 us
    all_to_all x1, waiting for transfers between devices, body(): lax.all_to_all(grouped, 'seq', split_axis=1, concat_axis=0, tiled=True)  36 us
    all_gather x1, waiting for transfers between devices, body(): weights_late = lax.all_gather(w_late, 'seq', axis=0, tiled=True)  35.7 us
    reduce_scatter x1, waiting for transfers between devices, body(): owned = lax.psum_scatter(products, 'seq', scatter_dimension=0, tiled=True)  26 us
    dot_general x4, matrix products, project(): jnp.dot(theirs, w_there, preferred_element_type=f32)  14.5 us
    ppermute x12, starting transfers between devices, in_block(): lax.ppermute(pieces[j], 'groups', swaps[j])  14.2 us
    dot_general x4, matrix products, project(): jnp.dot(ours, w_here, preferred_element_type=f32)  12.7 us
  transfers between devices with their start and end apart: 22, of which 20 were waited for; matrix products, arithmetic and copies ran while one was open for 17% of the time, Pallas kernels for 0%

profile of v2, /device:TPU:1604, one launch (start us, length us, event | category | flops | bytes accessed | tf_op | source)
XLA Modules:
  0.0 358.8 jit_solution(14627882442749696207)
XLA Ops:
  6.6 1.1 constant_dynamic-slice_fusion.1
  10.1 10.2 %convolution_convert_fusion.1 = bf16[384,1152]{1,0:T(8,128)(2,1)S(1)} fusion(bf16[2152,1152]{1,0:T(8,128)(2,1)} %param.12, bf16[1152,2152]{0,1:T(8,128)(2,1)} %param.11, bf16[384,1152]{1,0:T(8,128)(2,1)S(1)} %copy-done.1, f32[384]{0:T(512)S(1)} %add_rsqrt_fusion, f32[384]{0:T(512)S(1)} %broadcast_multiply_fusion), kind=kOutput, calls=%fused_computation.16 | convolution fusion | flops 3817552896 | bytes 11688960 | tf_op jit(solution)/shard_map/dot_general | solution.py:255
  21.8 9.4 %all-to-all-start = ((s32[16,1,288]{2,1,0:T(1,128)}), s32[16,1,288]{2,1,0:T(1,128)S(1)}, u32[]{:S(2)}, u32[]{:S(2)}) async-start(s32[16,1,288]{2,1,0:T(1,128)} %broadcast_in_dim.26), calls=%async_computation | async-start | bytes 49152 | tf_op jit(solution)/shard_map/all_to_all | solution.py:29
  31.3 1.4 fusion.98
  32.7 1.6 reshape.105
  35.2 2.5 fusion.43
  37.7 1.3 all-to-all-done
  39.1 10.7 %all-to-all-start.1 = ((bf16[48,16,288]{2,0,1:T(8,128)(2,1)}), bf16[48,16,288]{2,0,1:T(8,128)(2,1)S(1)}, u32[]{:S(2)}, u32[]{:S(2)}) async-start(bf16[48,16,288]{2,0,1:T(8,128)(2,1)} %fusion.43), calls=%async_computation.1 | async-start | bytes 1179648 | tf_op jit(solution)/shard_map/all_to_all | solution.py:265
  50.1 36.0 %all-to-all-done.1 = bf16[48,16,288]{2,0,1:T(8,128)(2,1)S(1)} async-done(((bf16[48,16,288]{2,0,1:T(8,128)(2,1)}), bf16[48,16,288]{2,0,1:T(8,128)(2,1)S(1)}, u32[]{:S(2)}, u32[]{:S(2)}) %all-to-all-start.1) | async-done | bytes 442400 | tf_op jit(solution)/shard_map/all_to_all | solution.py:265
  88.7 9.5 %convolution_convert_fusion = bf16[1536,2560]{1,0:T(8,128)(2,1)} fusion(bf16[288,2560]{1,0:T(8,128)(2,1)S(1)} %copy-done, s32[1536]{0:T(1024)S(1)} %convert_reduce_fusion, bf16[768,288]{1,0:T(8,128)(2,1)S(1)} %copy.17, bf16[768,288]{1,0:T(8,128)(2,1)S(1)} %bitcast.30), kind=kOutput, calls=%fused_computation | convolution fusion | flops 3632381952 | bytes 10229760 | tf_op jit(solution)/shard_map/dot_general | solution.py:276
  98.2 10.3 %all-gather.3.cloned.1.call-done = bf16[5120,512]{1,0:T(8,128)(2,1)} async-done(((bf16[320,512]{1,0:T(8,128)(2,1)}), bf16[5120,512]{1,0:T(8,128)(2,1)}) %all-gather.3.cloned.1.call-update) | async-done | bytes 5242896 | tf_op jit(solution)/shard_map/all_gather | solution.py:244
  108.7 1.6 collective-permute-start.2
  110.3 1.3 collective-permute-start.3
  113.3 19.0 %collective-permute-done.2 = bf16[192,2560]{1,0:T(8,128)(2,1)S(1)} collective-permute-done((bf16[192,2560]{1,0:T(8,128)(2,1)S(1)}, bf16[192,2560]{1,0:T(8,128)(2,1)S(1)}, u32[]{:S(2)}, u32[]{:S(2)}) %collective-permute-start.2) | collective-permute-done | bytes 983072 | tf_op jit(solution)/shard_map/ppermute | solution.py:231
  133.3 1.6 collective-permute-done.3
  135.9 12.8 %collective-permute-done.4 = bf16[192,2560]{1,0:T(8,128)(2,1)S(1)} collective-permute-done((bf16[192,2560]{1,0:T(8,128)(2,1)S(1)}, bf16[192,2560]{1,0:T(8,128)(2,1)S(1)}, u32[]{:S(2)}, u32[]{:S(2)}) %collective-permute-start.4) | collective-permute-done | bytes 983072 | tf_op jit(solution)/shard_map/ppermute | solution.py:231
  149.8 1.5 constant_dynamic-slice_fusion
  151.4 5.5 %collective-permute-done.5 = bf16[768,2560]{1,0:T(8,128)(2,1)} collective-permute-done((bf16[768,2560]{1,0:T(8,128)(2,1)}, bf16[768,2560]{1,0:T(8,128)(2,1)}, u32[]{:S(2)}, u32[]{:S(2)}) %collective-permute-start.5) | collective-permute-done | bytes 3932192 | tf_op jit(solution)/shard_map/ppermute | solution.py:35
  156.9 5.2 %fusion.14 = f32[768,512]{1,0:T(8,128)S(1)} fusion(bf16[768,2560]{1,0:T(8,128)(2,1)} %collective-permute-done.5, bf16[5120,512]{1,0:T(8,128)(2,1)} %all-gather.3.cloned.1.call-done, s32[]{:T(128)S(6)} %select_n.82), kind=kOutput, calls=%fused_computation.20 | convolution fusion | flops 2013265920 | bytes 8126468 | tf_op jit(solution)/shard_map/dot_general | solution.py:297
  162.1 4.3 %add_convert_fusion = bf16[768,512]{1,0:T(8,128)(2,1)S(1)} fusion(f32[768,512]{1,0:T(8,128)S(1)} %fusion.14, bf16[768,2560]{1,0:T(8,128)(2,1)} %constant_dynamic-update-slice_fusion.1, bf16[5120,512]{1,0:T(8,128)(2,1)S(1)} %bitcast.37, s32[]{:T(128)S(6)} %select_n.81), kind=kOutput, calls=%fused_computation.39 | convolution fusion | flops 2014052352 | bytes 8912900 | tf_op jit(solution)/shard_map/dot_general | solution.py:297
  167.3 1.6 collective-permute-start.6
  168.9 1.7 collective-permute-start.7
  171.1 3.3 collective-permute-done.6
  174.4 2.4 collective-permute-done.7
  176.9 2.9 collective-permute-done.8
  179.8 26.0 %reduce-scatter.2.cloned.1.call-done = bf16[96,2560]{1,0:T(8,128)(2,1)} async-done(((bf16[1536,2560]{1,0:T(8,128)(2,1)}), bf16[96,2560]{1,0:T(8,128)(2,1)}) %reduce-scatter.2.cloned.1.call-update) | async-done | bytes 491536 | tf_op jit(solution)/shard_map/reduce_scatter | solution.py:278
  205.8 1.5 collective-permute-start.9
  207.3 1.5 collective-permute-start.10
  208.8 1.8 constant_dynamic-update-slice_fusion.8
  211.2 8.0 %collective-permute-done.9 = bf16[96,2560]{1,0:T(8,128)(2,1)S(1)} collective-permute-done((bf16[96,2560]{1,0:T(8,128)(2,1)}, bf16[96,2560]{1,0:T(8,128)(2,1)S(1)}, u32[]{:S(2)}, u32[]{:S(2)}) %collective-permute-start.9) | collective-permute-done | bytes 491552 | tf_op jit(solution)/shard_map/ppermute | solution.py:231
  220.0 1.7 collective-permute-done.10
  221.7 1.8 constant_dynamic-update-slice_fusion.6
  223.6 7.1 %collective-permute-done.11 = bf16[96,2560]{1,0:T(8,128)(2,1)S(1)} collective-permute-done((bf16[96,2560]{1,0:T(8,128)(2,1)}, bf16[96,2560]{1,0:T(8,128)(2,1)S(1)}, u32[]{:S(2)}, u32[]{:S(2)}) %collective-permute-start.11) | collective-permute-done | bytes 491552 | tf_op jit(solution)/shard_map/ppermute | solution.py:231
  231.5 1.4 select_convert_fusion.doc_k_ref
  234.7 1.1 collective-permute-done.16
  235.8 35.7 %all-gather.5.cloned.1.call-done = bf16[5120,128]{1,0:T(8,128)(2,1)} async-done(((bf16[320,128]{1,0:T(8,128)(2,1)}), bf16[5120,128]{1,0:T(8,128)(2,1)}) %all-gather.5.cloned.1.call-update) | async-done | bytes 1310736 | tf_op jit(solution)/shard_map/all_gather | solution.py:307
  271.5 3.6 %fusion.58 = f32[768,128]{1,0:T(8,128)S(1)} fusion(bf16[768,2560]{1,0:T(8,128)(2,1)} %collective-permute-done.5, bf16[5120,128]{1,0:T(8,128)(2,1)} %all-gather.5.cloned.1.call-done, s32[]{:T(128)S(6)} %select_n.82), kind=kOutput, calls=%fused_computation.61 | convolution fusion | flops 503316480 | bytes 4980740 | tf_op jit(solution)/shard_map/dot_general | solution.py:297
  275.1 3.4 fusion.44
  278.5 3.5 fusion.12
  282.1 2.7 fusion.36
  284.8 2.2 fusion.60
  287.0 2.2 fusion.45
  289.5 1.6 collective-permute-start.13
  291.1 1.5 collective-permute-start.14
  293.1 1.9 collective-permute-done.13
  295.1 1.4 collective-permute-done.14
  296.5 2.3 collective-permute-done.15
  299.4 52.0 %attend.1 = bf16[192,2048]{1,0:T(8,128)(2,1)S(1)} custom-call(bf16[192,2560]{1,0:T(8,128)(2,1)S(1)} %multiply_convert_fusion.qkv_ref, bf16[192,128]{1,0:T(8,128)(2,1)S(1)} %fusion.74.doc_q_ref, bf16[3072,128]{1,0:T(8,128)(2,1)S(1)} %select_convert_fusion.doc_k_ref), custom_call_target="tpu_custom_call" | custom-call | flops 2717908992 | bytes 3932160 | tf_op jit(solution)/shard_map/attend/pallas_call | solution.py:183
  (125 shorter events, 20.4 us)
Async XLA Ops:
  6.5 82.2 %copy-start = (bf16[288,2560]{1,0:T(8,128)(2,1)S(1)}, bf16[288,2560]{1,0:T(8,128)(2,1)}, u32[]{:S(2)}) copy-start(bf16[288,2560]{1,0:T(8,128)(2,1)} %param.13) | copy-start | bytes 4423684
  6.6 2.9 copy-start.1
  6.6 102.0 %all-gather.3.cloned.1.call-start = ((), (), s32[]{:S(2)}) async-start(), calls=%async_computation.3 | async-start | bytes 5570560 | tf_op jit(solution)/shard_map/all_gather | solution.py:244
  10.1 11.1 %copy-start.13 = (s32[192]{0:T(256)S(1)}, s32[192]{0:T(256)}, u32[]{:S(2)}) copy-start(s32[192]{0:T(256)} %param.19) | copy-start | bytes 2308
  10.1 11.1 %copy-start.14 = (s32[96]{0:T(128)S(1)}, s32[96]{0:T(128)}, u32[]{:S(2)}) copy-start(s32[96]{0:T(128)} %param.18) | copy-start | bytes 1156
  20.3 11.0 %copy-start.4 = (bf16[384,1152]{1,0:T(8,128)(2,1)}, bf16[384,1152]{1,0:T(8,128)(2,1)S(1)}, u32[]{:S(2)}) copy-start(bf16[384,1152]{1,0:T(8,128)(2,1)S(1)} %convolution_convert_fusion.1) | copy-start | bytes 2654212
  21.1 10.1 %collective-permute-start = (bf16[192,1152]{1,0:T(8,128)(2,1)}, bf16[192,1152]{1,0:T(8,128)(2,1)}, u32[]{:S(2)}, u32[]{:S(2)}) collective-permute-start(bf16[192,1152]{1,0:T(8,128)(2,1)} %constant_dynamic-slice_fusion.2), channel_id=1, source_target_pairs={{0,1},{1,0},{2,3},{3,2},{4,5},{5,4},{6,7},{7,6},{8,9},{9,8},{10,11... | collective-permute-start | bytes 1327112 | tf_op jit(solution)/shard_map/ppermute | solution.py:35
  21.8 17.2 %all-to-all-start = ((s32[16,1,288]{2,1,0:T(1,128)}), s32[16,1,288]{2,1,0:T(1,128)S(1)}, u32[]{:S(2)}, u32[]{:S(2)}) async-start(s32[16,1,288]{2,1,0:T(1,128)} %broadcast_in_dim.26), calls=%async_computation | async-start | bytes 49152 | tf_op jit(solution)/shard_map/all_to_all | solution.py:29
  39.1 47.0 %all-to-all-start.1 = ((bf16[48,16,288]{2,0,1:T(8,128)(2,1)}), bf16[48,16,288]{2,0,1:T(8,128)(2,1)S(1)}, u32[]{:S(2)}, u32[]{:S(2)}) async-start(bf16[48,16,288]{2,0,1:T(8,128)(2,1)} %fusion.43), calls=%async_computation.1 | async-start | bytes 1179648 | tf_op jit(solution)/shard_map/all_to_all | solution.py:265
  49.8 156.0 %reduce-scatter.2.cloned.1.call-start = ((), (), s32[]{:S(2)}) async-start(), calls=%async_computation.4 | async-start | bytes 8355840 | tf_op jit(solution)/shard_map/reduce_scatter | solution.py:278
  86.3 2.1 collective-permute-start.1
  98.2 10.5 %copy-start.3 = (bf16[192,2560]{1,0:T(8,128)(2,1)S(1)}, bf16[192,2560]{1,0:T(8,128)(2,1)}, u32[]{:S(2)}) copy-start(bf16[192,2560]{1,0:T(8,128)(2,1)} %param.14) | copy-start | bytes 2949124
  108.6 162.9 %all-gather.5.cloned.1.call-start = ((), (), s32[]{:S(2)}) async-start(), calls=%async_computation.5 | async-start | bytes 1392640 | tf_op jit(solution)/shard_map/all_gather | solution.py:307
  108.7 23.6 %collective-permute-start.2 = (bf16[192,2560]{1,0:T(8,128)(2,1)S(1)}, bf16[192,2560]{1,0:T(8,128)(2,1)S(1)}, u32[]{:S(2)}, u32[]{:S(2)}) collective-permute-start(bf16[192,2560]{1,0:T(8,128)(2,1)S(1)} %copy-done.3), channel_id=1, source_target_pairs={{0,32},{32,0},{64,96},{96,64},{1,33},{33,1},{65,97},{97,65},{2,34}... | collective-permute-start | bytes 2949128 | tf_op jit(solution)/shard_map/ppermute | solution.py:231
  110.3 24.6 %collective-permute-start.3 = (bf16[192,2560]{1,0:T(8,128)(2,1)S(1)}, bf16[192,2560]{1,0:T(8,128)(2,1)S(1)}, u32[]{:S(2)}, u32[]{:S(2)}) collective-permute-start(bf16[192,2560]{1,0:T(8,128)(2,1)S(1)} %copy-done.3), channel_id=1, source_target_pairs={{0,64},{32,96},{64,0},{96,32},{1,65},{33,97},{65,1},{97,33},{2,66}... | collective-permute-start | bytes 2949128 | tf_op jit(solution)/shard_map/ppermute | solution.py:231
  111.6 37.1 %collective-permute-start.4 = (bf16[192,2560]{1,0:T(8,128)(2,1)S(1)}, bf16[192,2560]{1,0:T(8,128)(2,1)S(1)}, u32[]{:S(2)}, u32[]{:S(2)}) collective-permute-start(bf16[192,2560]{1,0:T(8,128)(2,1)S(1)} %copy-done.3), channel_id=1, source_target_pairs={{0,96},{32,64},{64,32},{96,0},{1,97},{33,65},{65,33},{97,1},{2,98}... | collective-permute-start | bytes 2949128 | tf_op jit(solution)/shard_map/ppermute | solution.py:231
  149.7 7.1 %collective-permute-start.5 = (bf16[768,2560]{1,0:T(8,128)(2,1)}, bf16[768,2560]{1,0:T(8,128)(2,1)}, u32[]{:S(2)}, u32[]{:S(2)}) collective-permute-start(bf16[768,2560]{1,0:T(8,128)(2,1)} %constant_dynamic-update-slice_fusion.1), channel_id=1, source_target_pairs={{0,1},{1,0},{2,3},{3,2},{4,5},{5,4},{6,7},{7,6},{8,9},{9,8},{10,11... | collective-permute-start | bytes 11796488 | tf_op jit(solution)/shard_map/ppermute | solution.py:35
  151.3 10.8 %slice-start = ((s8[5242880]{0:T(1024)(128)(4,1)}), s8[4194304]{0:T(1024)(128)(4,1)S(1)}, s32[]{:S(2)}) async-start(s8[5242880]{0:T(1024)(128)(4,1)} %bitcast.36), calls=%async_computation.6 | async-start | bytes 8388608
  151.4 10.7 %slice-start.1 = ((s8[5242880]{0:T(1024)(128)(4,1)}), s8[1048576]{0:T(1024)(128)(4,1)S(1)}, s32[]{:S(2)}) async-start(s8[5242880]{0:T(1024)(128)(4,1)} %bitcast.36), calls=%async_computation.7 | async-start | bytes 2097152
  167.3 7.1 %collective-permute-start.6 = (bf16[192,512]{1,0:T(8,128)(2,1)}, bf16[192,512]{1,0:T(8,128)(2,1)S(1)}, u32[]{:S(2)}, u32[]{:S(2)}) collective-permute-start(bf16[192,512]{1,0:T(8,128)(2,1)} %get-tuple-element.27), channel_id=1, source_target_pairs={{0,32},{32,0},{64,96},{96,64},{1,33},{33,1},{65,97},{97,65},{2,34}... | collective-permute-start | bytes 589832 | tf_op jit(solution)/shard_map/ppermute | solution.py:231
  168.9 8.0 %collective-permute-start.7 = (bf16[192,512]{1,0:T(8,128)(2,1)}, bf16[192,512]{1,0:T(8,128)(2,1)S(1)}, u32[]{:S(2)}, u32[]{:S(2)}) collective-permute-start(bf16[192,512]{1,0:T(8,128)(2,1)} %get-tuple-element.26), channel_id=1, source_target_pairs={{0,64},{32,96},{64,0},{96,32},{1,65},{33,97},{65,1},{97,33},{2,66}... | collective-permute-start | bytes 589832 | tf_op jit(solution)/shard_map/ppermute | solution.py:231
  170.5 9.3 %collective-permute-start.8 = (bf16[192,512]{1,0:T(8,128)(2,1)}, bf16[192,512]{1,0:T(8,128)(2,1)S(1)}, u32[]{:S(2)}, u32[]{:S(2)}) collective-permute-start(bf16[192,512]{1,0:T(8,128)(2,1)} %get-tuple-element.25), channel_id=1, source_target_pairs={{0,96},{32,64},{64,32},{96,0},{1,97},{33,65},{65,33},{97,1},{2,98}... | collective-permute-start | bytes 589832 | tf_op jit(solution)/shard_map/ppermute | solution.py:231
  174.4 31.4 %copy-start.10 = (bf16[192,512]{1,0:T(8,128)(2,1)}, bf16[192,512]{1,0:T(8,128)(2,1)S(1)}, u32[]{:S(2)}) copy-start(bf16[192,512]{1,0:T(8,128)(2,1)S(1)} %collective-permute-done.6) | copy-start | bytes 589828
  176.9 29.0 %copy-start.8 = (bf16[192,512]{1,0:T(8,128)(2,1)}, bf16[192,512]{1,0:T(8,128)(2,1)S(1)}, u32[]{:S(2)}) copy-start(bf16[192,512]{1,0:T(8,128)(2,1)S(1)} %collective-permute-done.7) | copy-start | bytes 589828
  179.8 26.0 %copy-start.6 = (bf16[192,512]{1,0:T(8,128)(2,1)}, bf16[192,512]{1,0:T(8,128)(2,1)S(1)}, u32[]{:S(2)}) copy-start(bf16[192,512]{1,0:T(8,128)(2,1)S(1)} %collective-permute-done.8) | copy-start | bytes 589828
  205.8 13.4 %collective-permute-start.9 = (bf16[96,2560]{1,0:T(8,128)(2,1)}, bf16[96,2560]{1,0:T(8,128)(2,1)S(1)}, u32[]{:S(2)}, u32[]{:S(2)}) collective-permute-start(bf16[96,2560]{1,0:T(8,128)(2,1)} %reduce-scatter.2.cloned.1.call-done), channel_id=1, source_target_pairs={{0,32},{32,0},{64,96},{96,64},{1,33},{33,1},{65,97},{97,65},{2,34}... | collective-permute-start | bytes 1474568 | tf_op jit(solution)/shard_map/ppermute | solution.py:231
  207.3 14.4 %collective-permute-start.10 = (bf16[96,2560]{1,0:T(8,128)(2,1)}, bf16[96,2560]{1,0:T(8,128)(2,1)}, u32[]{:S(2)}, u32[]{:S(2)}) collective-permute-start(bf16[96,2560]{1,0:T(8,128)(2,1)} %reduce-scatter.2.cloned.1.call-done), channel_id=1, source_target_pairs={{0,64},{32,96},{64,0},{96,32},{1,65},{33,97},{65,1},{97,33},{2,66}... | collective-permute-start | bytes 1474568 | tf_op jit(solution)/shard_map/ppermute | solution.py:231
  210.7 22.2 %copy-start.5 = (bf16[96,2560]{1,0:T(8,128)(2,1)S(1)}, bf16[96,2560]{1,0:T(8,128)(2,1)}, u32[]{:S(2)}) copy-start(bf16[96,2560]{1,0:T(8,128)(2,1)} %reduce-scatter.2.cloned.1.call-done) | copy-start | bytes 1474564
  210.7 20.0 %collective-permute-start.11 = (bf16[96,2560]{1,0:T(8,128)(2,1)}, bf16[96,2560]{1,0:T(8,128)(2,1)S(1)}, u32[]{:S(2)}, u32[]{:S(2)}) collective-permute-start(bf16[96,2560]{1,0:T(8,128)(2,1)} %reduce-scatter.2.cloned.1.call-done), channel_id=1, source_target_pairs={{0,96},{32,64},{64,32},{96,0},{1,97},{33,65},{65,33},{97,1},{2,98}... | collective-permute-start | bytes 1474568 | tf_op jit(solution)/shard_map/ppermute | solution.py:231
  231.5 47.0 %collective-permute-start.12 = (bf16[384,2560]{1,0:T(8,128)(2,1)}, bf16[384,2560]{1,0:T(8,128)(2,1)}, u32[]{:S(2)}, u32[]{:S(2)}) collective-permute-start(bf16[384,2560]{1,0:T(8,128)(2,1)} %constant_dynamic-update-slice_fusion.5), channel_id=1, source_target_pairs={{0,1},{1,0},{2,3},{3,2},{4,5},{5,4},{6,7},{7,6},{8,9},{9,8},{10,11... | collective-permute-start | bytes 5898248 | tf_op jit(solution)/shard_map/ppermute | solution.py:35
  233.4 2.4 collective-permute-start.16
  271.5 3.6 %copy-start.2 = (bf16[5120,128]{1,0:T(8,128)(2,1)S(1)}, bf16[5120,128]{1,0:T(8,128)(2,1)}, u32[]{:S(2)}) copy-start(bf16[5120,128]{1,0:T(8,128)(2,1)} %all-gather.5.cloned.1.call-done) | copy-start | bytes 3932164
  271.5 10.6 %slice-start.2 = ((s8[5242880]{0:T(1024)(128)(4,1)}), s8[4194304]{0:T(1024)(128)(4,1)S(1)}, s32[]{:S(2)}) async-start(s8[5242880]{0:T(1024)(128)(4,1)} %bitcast.38), calls=%async_computation.8 | async-start | bytes 8388608
  275.1 7.0 %slice-start.3 = ((s8[5242880]{0:T(1024)(128)(4,1)}), s8[1048576]{0:T(1024)(128)(4,1)S(1)}, s32[]{:S(2)}) async-start(s8[5242880]{0:T(1024)(128)(4,1)} %bitcast.38), calls=%async_computation.9 | async-start | bytes 2097152
  289.3 3.8 %copy-start.12 = (bf16[192,2560]{1,0:T(8,128)(2,1)S(1)}, bf16[192,2560]{1,0:T(8,128)(2,1)}, u32[]{:S(2)}) copy-start(bf16[192,2560]{1,0:T(8,128)(2,1)} %constant_dynamic-update-slice_fusion.12) | copy-start | bytes 2949124
  289.3 3.8 %copy-start.11 = (bf16[192,512]{1,0:T(8,128)(2,1)S(1)}, bf16[192,512]{1,0:T(8,128)(2,1)}, u32[]{:S(2)}) copy-start(bf16[192,512]{1,0:T(8,128)(2,1)} %copy-done.10) | copy-start | bytes 589828
  289.3 5.8 %copy-start.9 = (bf16[192,512]{1,0:T(8,128)(2,1)S(1)}, bf16[192,512]{1,0:T(8,128)(2,1)}, u32[]{:S(2)}) copy-start(bf16[192,512]{1,0:T(8,128)(2,1)} %copy-done.8) | copy-start | bytes 589828
  289.3 7.2 %copy-start.7 = (bf16[192,512]{1,0:T(8,128)(2,1)S(1)}, bf16[192,512]{1,0:T(8,128)(2,1)}, u32[]{:S(2)}) copy-start(bf16[192,512]{1,0:T(8,128)(2,1)} %copy-done.6) | copy-start | bytes 589828
  289.5 5.5 %collective-permute-start.13 = (bf16[96,896]{1,0:T(8,128)(2,1)S(1)}, bf16[96,896]{1,0:T(8,128)(2,1)S(1)}, u32[]{:S(2)}, u32[]{:S(2)}) collective-permute-start(bf16[96,896]{1,0:T(8,128)(2,1)S(1)} %get-tuple-element.31), channel_id=1, source_target_pairs={{0,32},{32,0},{64,96},{96,64},{1,33},{33,1},{65,97},{97,65},{2,34}... | collective-permute-start | bytes 516104 | tf_op jit(solution)/shard_map/ppermute | solution.py:231
  291.1 5.4 %collective-permute-start.14 = (bf16[96,896]{1,0:T(8,128)(2,1)S(1)}, bf16[96,896]{1,0:T(8,128)(2,1)S(1)}, u32[]{:S(2)}, u32[]{:S(2)}) collective-permute-start(bf16[96,896]{1,0:T(8,128)(2,1)S(1)} %get-tuple-element.30), channel_id=1, source_target_pairs={{0,64},{32,96},{64,0},{96,32},{1,65},{33,97},{65,1},{97,33},{2,66}... | collective-permute-start | bytes 516104 | tf_op jit(solution)/shard_map/ppermute | solution.py:231
  292.6 6.3 %collective-permute-start.15 = (bf16[96,896]{1,0:T(8,128)(2,1)S(1)}, bf16[96,896]{1,0:T(8,128)(2,1)S(1)}, u32[]{:S(2)}, u32[]{:S(2)}) collective-permute-start(bf16[96,896]{1,0:T(8,128)(2,1)S(1)} %get-tuple-element.29), channel_id=1, source_target_pairs={{0,96},{32,64},{64,32},{96,0},{1,97},{33,65},{65,33},{97,1},{2,98}... | collective-permute-start | bytes 516104 | tf_op jit(solution)/shard_map/ppermute | solution.py:231
Sparse Core Ops, SparseCore 0:
  9.6 98.9 all-gather.2
  111.0 94.7 reduce-scatter.1
  208.9 62.4 all-gather.4

commit v3 on v2

--- a/solution.py
+++ b/solution.py
@@ -239,9 +239,8 @@
         ],
         axis=1,
     )
-    late = HD
-    early = kv_part + q_part - late
-    weights = lax.all_gather(w_mine[:, :early], "seq", axis=0, tiled=True)
+    width = kv_part + q_part
+    weights = lax.all_gather(w_mine, "seq", axis=0, tiled=True)
 
     ints = everyones(jnp.concatenate([dest_rows, doc_ids]), "seq")
     merged_rows = dest_rows.shape[0]
@@ -299,39 +298,18 @@
         )
         return out.astype(bf16).reshape(BLOCK, -1, out.shape[1])
 
-    text_in = both_halves(in_block([text_states] * BLOCK))
-    text_out = project(text_in, weights)
+    text_out = project(both_halves(in_block([text_states] * BLOCK)), weights)
     text_out = in_block([text_out[j] for j in range(BLOCK)])
     owned, text_out = lax.optimization_barrier((owned, text_out))
-    w_late, owned = lax.optimization_barrier((w_mine[:, early:], owned))
-    weights_late = lax.all_gather(w_late, "seq", axis=0, tiled=True)
-    image_in = both_halves(in_block([owned] * BLOCK))
-    image_out = project(image_in, weights)
-    image_late = project(image_in, weights_late)
-    text_late = project(text_in, weights_late)
-    cut = text_rows // 2
-    back = jnp.concatenate(
-        [image_out, image_late, text_late[:, :cut], text_late[:, cut:]], axis=2
-    )
-    back = in_block([back[j] for j in range(BLOCK)])
+    image_out = project(both_halves(in_block([owned] * BLOCK)), weights)
+    image_out = in_block([image_out[j] for j in range(BLOCK)])
 
     mixed = text_states.astype(f32) + jnp.dot(placer, owned, preferred_element_type=f32)
     squares = jnp.sum(mixed * mixed, axis=1)
     squares = squares + swap_core(squares)
     scale = lax.rsqrt(squares / (2 * half_width) + epsilon)[:, None]
-    width = early + late
-    from_image = jnp.concatenate([p[:, :width] for p in back], axis=1)
-    from_text = jnp.concatenate(
-        [
-            x
-            for t, p in zip(text_out, back)
-            for x in (
-                t,
-                jnp.concatenate([p[:, width : width + late], p[:, width + late :]], axis=0),
-            )
-        ],
-        axis=1,
-    )
+    from_image = jnp.concatenate(image_out, axis=1)
+    from_text = jnp.concatenate(text_out, axis=1)
     is_query = jnp.arange(BLOCK * width) % width >= kv_part
     soft = jnp.where(is_query, HD ** (-0.5) * LOG2E, 1.0)[None, :].astype(f32)
     qkv = (

time: 362 us -> 327 us (0.903)
  waiting for transfers between devices: 181 us -> 154 us
  matrix products: 47.8 us -> 42.9 us
    all_gather x2 -> x1, waiting for transfers between devices: 46 us -> 19.1 us  [body(): weights = lax.all_gather(w_mine, 'seq', axis=0, tiled=True)]
    reduce_scatter x1, waiting for transfers between devices: 26 us -> 16.2 us  [body(): owned = lax.psum_scatter(products, 'seq', scatter_dimension=0, tiled=True)]
    ppermute x12, waiting for transfers between devices: 64.4 us -> 73.3 us  [in_block(): lax.ppermute(pieces[j], 'groups', swaps[j])]
    dot_general x4 -> x2, matrix products: 14.5 us -> 10.6 us  [project(): jnp.dot(theirs, w_there, preferred_element_type=f32)]
    dot_general x4 -> x2, matrix products: 12.7 us -> 10.7 us  [project(): jnp.dot(ours, w_here, preferred_element_type=f32)]
    unnamed x51 -> x31, local copies, waits for them, and re-layouts: 9.29 us -> 8.25 us
  transfers between devices with their start and end apart: 22 -> 21, of which waited for: 20 -> 18; matrix products, arithmetic and copies ran while one was open for 17% -> 19% of each run, Pallas kernels for 0% -> 0%
where the time goes in v3:
time: 327 us; the launch traced here: 325 us
  waiting for transfers between devices  154 us (47%)
  Pallas kernels  52.9 us (16%)
  matrix products  42.9 us (13%)
  starting transfers between devices  35.7 us (11%)
  local copies, waits for them, and re-layouts  16.7 us (5%)
  between operations  13.7 us (4%)
  other arithmetic  9.11 us (3%)
    ppermute x12, waiting for transfers between devices, in_block(): lax.ppermute(pieces[j], 'groups', swaps[j])  73.3 us
    pallas_call x1, Pallas kernels, attention(): pl.pallas_call(functools.partial(attention_kernel, reach, kv_local, group...  52.9 us
    all_to_all x1, waiting for transfers between devices, body(): lax.all_to_all(grouped, 'seq', split_axis=1, concat_axis=0, tiled=True)  35.4 us
    all_gather x1, waiting for transfers between devices, body(): weights = lax.all_gather(w_mine, 'seq', axis=0, tiled=True)  19.1 us
    reduce_scatter x1, waiting for transfers between devices, body(): owned = lax.psum_scatter(products, 'seq', scatter_dimension=0, tiled=True)  16.2 us
    ppermute x12, starting transfers between devices, in_block(): lax.ppermute(pieces[j], 'groups', swaps[j])  14.3 us
    all_to_all x1, starting transfers between devices, body(): lax.all_to_all(grouped, 'seq', split_axis=1, concat_axis=0, tiled=True)  11 us
    dot_general x2, matrix products, project(): jnp.dot(ours, w_here, preferred_element_type=f32)  10.7 us
  transfers between devices with their start and end apart: 21, of which 18 were waited for; matrix products, arithmetic and copies ran while one was open for 19% of the time, Pallas kernels for 0%

profile of v3, /device:TPU:1604, one launch (start us, length us, event | category | flops | bytes accessed | tf_op | source)
XLA Modules:
  0.0 325.3 jit_solution(10227208492296373498)
XLA Ops:
  6.6 1.1 constant_dynamic-slice_fusion
  7.7 0.9 fusion.67
  10.2 10.2 %convolution_convert_fusion.1 = bf16[384,1152]{1,0:T(8,128)(2,1)S(1)} fusion(bf16[2152,1152]{1,0:T(8,128)(2,1)} %param.12, bf16[1152,2152]{0,1:T(8,128)(2,1)} %param.11, bf16[384,1152]{1,0:T(8,128)(2,1)S(1)} %copy-done.1, f32[384]{0:T(512)S(1)} %add_rsqrt_fusion, f32[384]{0:T(512)S(1)} %broadcast_multiply_fusion), kind=kOutput, calls=%fused_computation.28 | convolution fusion | flops 3817552896 | bytes 11688960 | tf_op jit(solution)/shard_map/dot_general | solution.py:254
  20.4 0.9 constant_dynamic-slice_fusion.1
  21.9 9.4 %all-to-all-start = ((s32[16,1,288]{2,1,0:T(1,128)}), s32[16,1,288]{2,1,0:T(1,128)}, u32[]{:S(2)}, u32[]{:S(2)}) async-start(s32[16,1,288]{2,1,0:T(1,128)} %broadcast_in_dim.26), calls=%async_computation | async-start | bytes 49152 | tf_op jit(solution)/shard_map/all_to_all | solution.py:29
  31.4 1.4 fusion.86
  34.1 0.8 reduce_sum.82
  37.0 1.2 fusion.46
  38.2 1.1 all-to-all-done
  39.3 11.0 %all-to-all-start.1 = ((bf16[48,16,288]{2,0,1:T(8,128)(2,1)}), bf16[48,16,288]{2,0,1:T(8,128)(2,1)S(1)}, u32[]{:S(2)}, u32[]{:S(2)}) async-start(bf16[48,16,288]{2,0,1:T(8,128)(2,1)} %fusion.46), calls=%async_computation.1 | async-start | bytes 1179648 | tf_op jit(solution)/shard_map/all_to_all | solution.py:264
  51.3 35.4 %all-to-all-done.1 = bf16[48,16,288]{2,0,1:T(8,128)(2,1)S(1)} async-done(((bf16[48,16,288]{2,0,1:T(8,128)(2,1)}), bf16[48,16,288]{2,0,1:T(8,128)(2,1)S(1)}, u32[]{:S(2)}, u32[]{:S(2)}) %all-to-all-start.1) | async-done | bytes 442400 | tf_op jit(solution)/shard_map/all_to_all | solution.py:264
  87.2 1.1 convert_reduce_fusion
  89.3 9.5 %convolution_convert_fusion = bf16[1536,2560]{1,0:T(8,128)(2,1)} fusion(bf16[288,2560]{1,0:T(8,128)(2,1)S(1)} %copy-done, s32[1536]{0:T(1024)S(1)} %convert_reduce_fusion, bf16[768,288]{1,0:T(8,128)(2,1)S(1)} %copy.17, bf16[768,288]{1,0:T(8,128)(2,1)S(1)} %bitcast.15), kind=kOutput, calls=%fused_computation | convolution fusion | flops 3632381952 | bytes 10229760 | tf_op jit(solution)/shard_map/dot_general | solution.py:275
  98.8 19.1 %all-gather.2.cloned.1.call-done = bf16[5120,640]{1,0:T(8,128)(2,1)} async-done(((bf16[320,640]{1,0:T(8,128)(2,1)}), bf16[5120,640]{1,0:T(8,128)(2,1)}) %all-gather.2.cloned.1.call-update) | async-done | bytes 6553616 | tf_op jit(solution)/shard_map/all_gather | solution.py:243
  118.0 1.6 collective-permute-start.2
  119.6 1.5 collective-permute-start.3
  121.6 1.0 constant_dynamic-update-slice_fusion.4
  122.6 19.2 %collective-permute-done.2 = bf16[192,2560]{1,0:T(8,128)(2,1)S(1)} collective-permute-done((bf16[192,2560]{1,0:T(8,128)(2,1)S(1)}, bf16[192,2560]{1,0:T(8,128)(2,1)S(1)}, u32[]{:S(2)}, u32[]{:S(2)}) %collective-permute-start.2) | collective-permute-done | bytes 983072 | tf_op jit(solution)/shard_map/ppermute | solution.py:231
  141.8 1.0 constant_dynamic-update-slice_fusion.3
  142.9 1.3 collective-permute-done.3
  144.2 1.0 constant_dynamic-update-slice_fusion.2
  145.2 18.4 %collective-permute-done.4 = bf16[192,2560]{1,0:T(8,128)(2,1)S(1)} collective-permute-done((bf16[192,2560]{1,0:T(8,128)(2,1)S(1)}, bf16[192,2560]{1,0:T(8,128)(2,1)S(1)}, u32[]{:S(2)}, u32[]{:S(2)}) %collective-permute-start.4) | collective-permute-done | bytes 983072 | tf_op jit(solution)/shard_map/ppermute | solution.py:231
  163.7 1.0 constant_dynamic-update-slice_fusion.1
  164.7 7.1 %collective-permute-done.5 = bf16[768,2560]{1,0:T(8,128)(2,1)} collective-permute-done((bf16[768,2560]{1,0:T(8,128)(2,1)}, bf16[768,2560]{1,0:T(8,128)(2,1)}, u32[]{:S(2)}, u32[]{:S(2)}) %collective-permute-start.5) | collective-permute-done | bytes 3932192 | tf_op jit(solution)/shard_map/ppermute | solution.py:35
  171.8 6.4 %fusion.16 = f32[768,640]{1,0:T(8,128)S(1)} fusion(bf16[768,2560]{1,0:T(8,128)(2,1)} %collective-permute-done.5, bf16[5120,640]{1,0:T(8,128)(2,1)} %all-gather.2.cloned.1.call-done, s32[]{:T(128)S(6)} %select_n.78), kind=kOutput, calls=%fused_computation.22 | convolution fusion | flops 2516582400 | bytes 9175044 | tf_op jit(solution)/shard_map/dot_general | solution.py:296
  178.2 6.4 %add_convert_fusion = bf16[768,640]{1,0:T(8,128)(2,1)S(1)} fusion(f32[768,640]{1,0:T(8,128)S(1)} %fusion.16, bf16[768,2560]{1,0:T(8,128)(2,1)} %constant_dynamic-update-slice_fusion.1, bf16[5120,640]{1,0:T(8,128)(2,1)} %all-gather.2.cloned.1.call-done, s32[]{:T(128)S(6)} %select_n.77), kind=kOutput, calls=%fused_computation.34 | convolution fusion | flops 2517565440 | bytes 10158084 | tf_op jit(solution)/shard_map/dot_general | solution.py:296
  184.8 1.6 collective-permute-start.6
  186.4 1.5 collective-permute-start.7
  188.4 4.5 %collective-permute-done.6 = bf16[192,640]{1,0:T(8,128)(2,1)S(1)} collective-permute-done((bf16[192,640]{1,0:T(8,128)(2,1)S(1)}, bf16[192,640]{1,0:T(8,128)(2,1)S(1)}, u32[]{:S(2)}, u32[]{:S(2)}) %collective-permute-start.6) | collective-permute-done | bytes 245792 | tf_op jit(solution)/shard_map/ppermute | solution.py:231
  192.8 2.3 collective-permute-done.7
  195.2 4.2 %collective-permute-done.8 = bf16[192,640]{1,0:T(8,128)(2,1)} collective-permute-done((bf16[192,640]{1,0:T(8,128)(2,1)S(1)}, bf16[192,640]{1,0:T(8,128)(2,1)}, u32[]{:S(2)}, u32[]{:S(2)}) %collective-permute-start.8) | collective-permute-done | bytes 245792 | tf_op jit(solution)/shard_map/ppermute | solution.py:231
  199.4 16.2 %reduce-scatter.2.cloned.1.call-done = bf16[96,2560]{1,0:T(8,128)(2,1)} async-done(((bf16[1536,2560]{1,0:T(8,128)(2,1)}), bf16[96,2560]{1,0:T(8,128)(2,1)}) %reduce-scatter.2.cloned.1.call-update) | async-done | bytes 491536 | tf_op jit(solution)/shard_map/reduce_scatter | solution.py:277
  215.6 1.5 collective-permute-start.9
  217.1 1.5 collective-permute-start.10
  218.6 1.9 constant_dynamic-update-slice_fusion.8
  221.0 8.0 %collective-permute-done.9 = bf16[96,2560]{1,0:T(8,128)(2,1)S(1)} collective-permute-done((bf16[96,2560]{1,0:T(8,128)(2,1)}, bf16[96,2560]{1,0:T(8,128)(2,1)S(1)}, u32[]{:S(2)}, u32[]{:S(2)}) %collective-permute-start.9) | collective-permute-done | bytes 491552 | tf_op jit(solution)/shard_map/ppermute | solution.py:231
  229.8 1.6 collective-permute-done.10
  232.2 8.2 %collective-permute-done.11 = bf16[96,2560]{1,0:T(8,128)(2,1)S(1)} collective-permute-done((bf16[96,2560]{1,0:T(8,128)(2,1)}, bf16[96,2560]{1,0:T(8,128)(2,1)S(1)}, u32[]{:S(2)}, u32[]{:S(2)}) %collective-permute-start.11) | collective-permute-done | bytes 491552 | tf_op jit(solution)/shard_map/ppermute | solution.py:231
  241.8 1.4 select_convert_fusion.doc_k_ref
  244.3 1.3 collective-permute-done.12
  245.6 4.2 %fusion.14 = f32[384,640]{1,0:T(8,128)S(1)} fusion(bf16[384,2560]{1,0:T(8,128)(2,1)} %collective-permute-done.12, bf16[5120,640]{1,0:T(8,128)(2,1)} %all-gather.2.cloned.1.call-done, s32[]{:T(128)S(6)} %select_n.78), kind=kOutput, calls=%fused_computation.20 | convolution fusion | flops 1258291200 | bytes 6225924 | tf_op jit(solution)/shard_map/dot_general | solution.py:296
  249.8 4.3 %fusion.39 = bf16[384,640]{1,0:T(8,128)(2,1)S(1)} fusion(f32[384,640]{1,0:T(8,128)S(1)} %fusion.14, bf16[384,2560]{1,0:T(8,128)(2,1)} %constant_dynamic-update-slice_fusion.5, bf16[5120,640]{1,0:T(8,128)(2,1)} %all-gather.2.cloned.1.call-done, s32[]{:T(128)S(6)} %select_n.77), kind=kOutput, calls=%fused_computation.46 | convolution fusion | flops 1258782720 | bytes 6717444 | tf_op jit(solution)/shard_map/dot_general | solution.py:296
  254.1 2.5 collective-permute-start.15
  257.7 3.6 %collective-permute-done.15 = bf16[96,640]{1,0:T(8,128)(2,1)S(1)} collective-permute-done((bf16[96,640]{1,0:T(8,128)(2,1)S(1)}, bf16[96,640]{1,0:T(8,128)(2,1)S(1)}, u32[]{:S(2)}, u32[]{:S(2)}) %collective-permute-start.15) | collective-permute-done | bytes 122912 | tf_op jit(solution)/shard_map/ppermute | solution.py:231
  261.3 1.8 collective-permute-done.14
  263.2 1.4 fusion.5.qkv_ref
  264.6 52.9 %attend.1 = bf16[192,2048]{1,0:T(8,128)(2,1)S(1)} custom-call(bf16[192,2560]{1,0:T(8,128)(2,1)S(1)} %fusion.5.qkv_ref, bf16[192,128]{1,0:T(8,128)(2,1)S(1)} %fusion.66.doc_q_ref, bf16[3072,128]{1,0:T(8,128)(2,1)S(1)} %select_convert_fusion.doc_k_ref), custom_call_target="tpu_custom_call" | custom-call | flops 2717908992 | bytes 3932160 | tf_op jit(solution)/shard_map/attend/pallas_call | solution.py:183
  317.5 0.9 copy.35
  (81 shorter events, 15.0 us)
Async XLA Ops:
  6.5 82.7 %copy-start = (bf16[288,2560]{1,0:T(8,128)(2,1)S(1)}, bf16[288,2560]{1,0:T(8,128)(2,1)}, u32[]{:S(2)}) copy-start(bf16[288,2560]{1,0:T(8,128)(2,1)} %param.13) | copy-start | bytes 4423684
  6.6 3.0 copy-start.1
  6.6 111.4 %all-gather.2.cloned.1.call-start = ((), (), s32[]{:S(2)}) async-start(), calls=%async_computation.3 | async-start | bytes 6963200 | tf_op jit(solution)/shard_map/all_gather | solution.py:243
  10.1 11.1 %copy-start.5 = (s32[192]{0:T(256)S(1)}, s32[192]{0:T(256)}, u32[]{:S(2)}) copy-start(s32[192]{0:T(256)} %param.19) | copy-start | bytes 2308
  10.1 11.1 %copy-start.6 = (s32[96]{0:T(128)S(1)}, s32[96]{0:T(128)}, u32[]{:S(2)}) copy-start(s32[96]{0:T(128)} %param.18) | copy-start | bytes 1156
  20.3 11.0 %copy-start.3 = (bf16[384,1152]{1,0:T(8,128)(2,1)}, bf16[384,1152]{1,0:T(8,128)(2,1)S(1)}, u32[]{:S(2)}) copy-start(bf16[384,1152]{1,0:T(8,128)(2,1)S(1)} %convolution_convert_fusion.1) | copy-start | bytes 2654212
  21.2 10.1 %collective-permute-start = (bf16[192,1152]{1,0:T(8,128)(2,1)}, bf16[192,1152]{1,0:T(8,128)(2,1)}, u32[]{:S(2)}, u32[]{:S(2)}) collective-permute-start(bf16[192,1152]{1,0:T(8,128)(2,1)} %constant_dynamic-slice_fusion.1), channel_id=1, source_target_pairs={{0,1},{1,0},{2,3},{3,2},{4,5},{5,4},{6,7},{7,6},{8,9},{9,8},{10,11... | collective-permute-start | bytes 1327112 | tf_op jit(solution)/shard_map/ppermute | solution.py:35
  21.9 17.3 %all-to-all-start = ((s32[16,1,288]{2,1,0:T(1,128)}), s32[16,1,288]{2,1,0:T(1,128)}, u32[]{:S(2)}, u32[]{:S(2)}) async-start(s32[16,1,288]{2,1,0:T(1,128)} %broadcast_in_dim.26), calls=%async_computation | async-start | bytes 49152 | tf_op jit(solution)/shard_map/all_to_all | solution.py:29
  39.3 47.4 %all-to-all-start.1 = ((bf16[48,16,288]{2,0,1:T(8,128)(2,1)}), bf16[48,16,288]{2,0,1:T(8,128)(2,1)S(1)}, u32[]{:S(2)}, u32[]{:S(2)}) async-start(bf16[48,16,288]{2,0,1:T(8,128)(2,1)} %fusion.46), calls=%async_computation.1 | async-start | bytes 1179648 | tf_op jit(solution)/shard_map/all_to_all | solution.py:264
  50.3 165.4 %reduce-scatter.2.cloned.1.call-start = ((), (), s32[]{:S(2)}) async-start(), calls=%async_computation.4 | async-start | bytes 8355840 | tf_op jit(solution)/shard_map/reduce_scatter | solution.py:277
  86.9 2.1 collective-permute-start.1
  98.8 19.2 %copy-start.2 = (bf16[192,2560]{1,0:T(8,128)(2,1)S(1)}, bf16[192,2560]{1,0:T(8,128)(2,1)}, u32[]{:S(2)}) copy-start(bf16[192,2560]{1,0:T(8,128)(2,1)} %param.14) | copy-start | bytes 2949124
  118.0 23.8 %collective-permute-start.2 = (bf16[192,2560]{1,0:T(8,128)(2,1)S(1)}, bf16[192,2560]{1,0:T(8,128)(2,1)S(1)}, u32[]{:S(2)}, u32[]{:S(2)}) collective-permute-start(bf16[192,2560]{1,0:T(8,128)(2,1)S(1)} %copy-done.2), channel_id=1, source_target_pairs={{0,32},{32,0},{64,96},{96,64},{1,33},{33,1},{65,97},{97,65},{2,34}... | collective-permute-start | bytes 2949128 | tf_op jit(solution)/shard_map/ppermute | solution.py:231
  119.6 24.6 %collective-permute-start.3 = (bf16[192,2560]{1,0:T(8,128)(2,1)S(1)}, bf16[192,2560]{1,0:T(8,128)(2,1)S(1)}, u32[]{:S(2)}, u32[]{:S(2)}) collective-permute-start(bf16[192,2560]{1,0:T(8,128)(2,1)S(1)} %copy-done.2), channel_id=1, source_target_pairs={{0,64},{32,96},{64,0},{96,32},{1,65},{33,97},{65,1},{97,33},{2,66}... | collective-permute-start | bytes 2949128 | tf_op jit(solution)/shard_map/ppermute | solution.py:231
  121.1 42.6 %collective-permute-start.4 = (bf16[192,2560]{1,0:T(8,128)(2,1)S(1)}, bf16[192,2560]{1,0:T(8,128)(2,1)S(1)}, u32[]{:S(2)}, u32[]{:S(2)}) collective-permute-start(bf16[192,2560]{1,0:T(8,128)(2,1)S(1)} %copy-done.2), channel_id=1, source_target_pairs={{0,96},{32,64},{64,32},{96,0},{1,97},{33,65},{65,33},{97,1},{2,98}... | collective-permute-start | bytes 2949128 | tf_op jit(solution)/shard_map/ppermute | solution.py:231
  164.7 7.1 %collective-permute-start.5 = (bf16[768,2560]{1,0:T(8,128)(2,1)}, bf16[768,2560]{1,0:T(8,128)(2,1)}, u32[]{:S(2)}, u32[]{:S(2)}) collective-permute-start(bf16[768,2560]{1,0:T(8,128)(2,1)} %constant_dynamic-update-slice_fusion.1), channel_id=1, source_target_pairs={{0,1},{1,0},{2,3},{3,2},{4,5},{5,4},{6,7},{7,6},{8,9},{9,8},{10,11... | collective-permute-start | bytes 11796488 | tf_op jit(solution)/shard_map/ppermute | solution.py:35
  184.8 8.1 %collective-permute-start.6 = (bf16[192,640]{1,0:T(8,128)(2,1)S(1)}, bf16[192,640]{1,0:T(8,128)(2,1)S(1)}, u32[]{:S(2)}, u32[]{:S(2)}) collective-permute-start(bf16[192,640]{1,0:T(8,128)(2,1)S(1)} %get-tuple-element.23), channel_id=1, source_target_pairs={{0,32},{32,0},{64,96},{96,64},{1,33},{33,1},{65,97},{97,65},{2,34}... | collective-permute-start | bytes 737288 | tf_op jit(solution)/shard_map/ppermute | solution.py:231
  186.4 8.8 %collective-permute-start.7 = (bf16[192,640]{1,0:T(8,128)(2,1)S(1)}, bf16[192,640]{1,0:T(8,128)(2,1)S(1)}, u32[]{:S(2)}, u32[]{:S(2)}) collective-permute-start(bf16[192,640]{1,0:T(8,128)(2,1)S(1)} %get-tuple-element.22), channel_id=1, source_target_pairs={{0,64},{32,96},{64,0},{96,32},{1,65},{33,97},{65,1},{97,33},{2,66}... | collective-permute-start | bytes 737288 | tf_op jit(solution)/shard_map/ppermute | solution.py:231
  187.8 11.6 %collective-permute-start.8 = (bf16[192,640]{1,0:T(8,128)(2,1)S(1)}, bf16[192,640]{1,0:T(8,128)(2,1)}, u32[]{:S(2)}, u32[]{:S(2)}) collective-permute-start(bf16[192,640]{1,0:T(8,128)(2,1)S(1)} %get-tuple-element.21), channel_id=1, source_target_pairs={{0,96},{32,64},{64,32},{96,0},{1,97},{33,65},{65,33},{97,1},{2,98}... | collective-permute-start | bytes 737288 | tf_op jit(solution)/shard_map/ppermute | solution.py:231
  192.8 25.7 %copy-start.7 = (bf16[192,640]{1,0:T(8,128)(2,1)}, bf16[192,640]{1,0:T(8,128)(2,1)S(1)}, u32[]{:S(2)}) copy-start(bf16[192,640]{1,0:T(8,128)(2,1)S(1)} %collective-permute-done.6) | copy-start | bytes 737284
  195.2 23.4 %copy-start.9 = (bf16[192,640]{1,0:T(8,128)(2,1)}, bf16[192,640]{1,0:T(8,128)(2,1)S(1)}, u32[]{:S(2)}) copy-start(bf16[192,640]{1,0:T(8,128)(2,1)S(1)} %collective-permute-done.7) | copy-start | bytes 737284
  215.6 13.4 %collective-permute-start.9 = (bf16[96,2560]{1,0:T(8,128)(2,1)}, bf16[96,2560]{1,0:T(8,128)(2,1)S(1)}, u32[]{:S(2)}, u32[]{:S(2)}) collective-permute-start(bf16[96,2560]{1,0:T(8,128)(2,1)} %reduce-scatter.2.cloned.1.call-done), channel_id=1, source_target_pairs={{0,32},{32,0},{64,96},{96,64},{1,33},{33,1},{65,97},{97,65},{2,34}... | collective-permute-start | bytes 1474568 | tf_op jit(solution)/shard_map/ppermute | solution.py:231
  217.1 14.3 %collective-permute-start.10 = (bf16[96,2560]{1,0:T(8,128)(2,1)}, bf16[96,2560]{1,0:T(8,128)(2,1)S(1)}, u32[]{:S(2)}, u32[]{:S(2)}) collective-permute-start(bf16[96,2560]{1,0:T(8,128)(2,1)} %reduce-scatter.2.cloned.1.call-done), channel_id=1, source_target_pairs={{0,64},{32,96},{64,0},{96,32},{1,65},{33,97},{65,1},{97,33},{2,66}... | collective-permute-start | bytes 1474568 | tf_op jit(solution)/shard_map/ppermute | solution.py:231
  220.4 22.7 %copy-start.4 = (bf16[96,2560]{1,0:T(8,128)(2,1)S(1)}, bf16[96,2560]{1,0:T(8,128)(2,1)}, u32[]{:S(2)}) copy-start(bf16[96,2560]{1,0:T(8,128)(2,1)} %reduce-scatter.2.cloned.1.call-done) | copy-start | bytes 1474564
  220.4 20.0 %collective-permute-start.11 = (bf16[96,2560]{1,0:T(8,128)(2,1)}, bf16[96,2560]{1,0:T(8,128)(2,1)S(1)}, u32[]{:S(2)}, u32[]{:S(2)}) collective-permute-start(bf16[96,2560]{1,0:T(8,128)(2,1)} %reduce-scatter.2.cloned.1.call-done), channel_id=1, source_target_pairs={{0,96},{32,64},{64,32},{96,0},{1,97},{33,65},{65,33},{97,1},{2,98}... | collective-permute-start | bytes 1474568 | tf_op jit(solution)/shard_map/ppermute | solution.py:231
  241.2 4.3 %collective-permute-start.12 = (bf16[384,2560]{1,0:T(8,128)(2,1)}, bf16[384,2560]{1,0:T(8,128)(2,1)}, u32[]{:S(2)}, u32[]{:S(2)}) collective-permute-start(bf16[384,2560]{1,0:T(8,128)(2,1)} %constant_dynamic-update-slice_fusion.5), channel_id=1, source_target_pairs={{0,1},{1,0},{2,3},{3,2},{4,5},{5,4},{6,7},{7,6},{8,9},{9,8},{10,11... | collective-permute-start | bytes 5898248 | tf_op jit(solution)/shard_map/ppermute | solution.py:35
  243.7 14.0 %collective-permute-start.16 = (f32[192]{0:T(256)S(1)}, f32[192]{0:T(256)S(1)}, u32[]{:S(2)}, u32[]{:S(2)}) collective-permute-start(f32[192]{0:T(256)S(1)} %fusion.35), channel_id=1, source_target_pairs={{0,1},{1,0},{2,3},{3,2},{4,5},{5,4},{6,7},{7,6},{8,9},{9,8},{10,11... | collective-permute-start | bytes 2312 | tf_op jit(solution)/shard_map/ppermute | solution.py:35
  249.8 13.4 %copy-start.8 = (bf16[192,640]{1,0:T(8,128)(2,1)S(1)}, bf16[192,640]{1,0:T(8,128)(2,1)}, u32[]{:S(2)}) copy-start(bf16[192,640]{1,0:T(8,128)(2,1)} %copy-done.7) | copy-start | bytes 737284
  249.8 13.4 %copy-start.10 = (bf16[192,640]{1,0:T(8,128)(2,1)S(1)}, bf16[192,640]{1,0:T(8,128)(2,1)}, u32[]{:S(2)}) copy-start(bf16[192,640]{1,0:T(8,128)(2,1)} %copy-done.9) | copy-start | bytes 737284
  254.1 7.2 %collective-permute-start.15 = (bf16[96,640]{1,0:T(8,128)(2,1)S(1)}, bf16[96,640]{1,0:T(8,128)(2,1)S(1)}, u32[]{:S(2)}, u32[]{:S(2)}) collective-permute-start(bf16[96,640]{1,0:T(8,128)(2,1)S(1)} %get-tuple-element.26), channel_id=1, source_target_pairs={{0,96},{32,64},{64,32},{96,0},{1,97},{33,65},{65,33},{97,1},{2,98}... | collective-permute-start | bytes 368648 | tf_op jit(solution)/shard_map/ppermute | solution.py:231
  256.6 6.5 %collective-permute-start.14 = (bf16[96,640]{1,0:T(8,128)(2,1)S(1)}, bf16[96,640]{1,0:T(8,128)(2,1)S(1)}, u32[]{:S(2)}, u32[]{:S(2)}) collective-permute-start(bf16[96,640]{1,0:T(8,128)(2,1)S(1)} %get-tuple-element.27), channel_id=1, source_target_pairs={{0,64},{32,96},{64,0},{96,32},{1,65},{33,97},{65,1},{97,33},{2,66}... | collective-permute-start | bytes 368648 | tf_op jit(solution)/shard_map/ppermute | solution.py:231
  257.2 6.0 %collective-permute-start.13 = (bf16[96,640]{1,0:T(8,128)(2,1)S(1)}, bf16[96,640]{1,0:T(8,128)(2,1)S(1)}, u32[]{:S(2)}, u32[]{:S(2)}) collective-permute-start(bf16[96,640]{1,0:T(8,128)(2,1)S(1)} %get-tuple-element.28), channel_id=1, source_target_pairs={{0,32},{32,0},{64,96},{96,64},{1,33},{33,1},{65,97},{97,65},{2,34}... | collective-permute-start | bytes 368648 | tf_op jit(solution)/shard_map/ppermute | solution.py:231
Sparse Core Ops, SparseCore 0:
  9.7 108.2 all-gather.1
  120.4 95.2 reduce-scatter.1
